TPU v7x, 512 devices: a whole 4x8x8 slice. The times are simulated.
512 devices in a mesh: gx: 8 (over x, core), gy: 64 (over y, z).
Axes of the slice: x: 4, y: 8, z: 8, core: 2. Of those that a mesh axis runs over, the one named last changes fastest.
Arguments:
- trial: float32 [786432, 384], P(('gx', 'gy')), may hold values from -30 to 30
- resid: float32 [786432, 128], P(('gx', 'gy')), may hold values from -500 to 500
- energy: float32 [786432], P(('gx', 'gy')), may hold values from 1 to 10
- shift: float32 [128], replicated, may hold values from 0.05 to 0.5
Outputs:
- basis: float32 [786432, 128], P(('gx', 'gy'))
All inputs are finite; a program needn't handle non-finite values.
Results may differ from a plain program's by a relative error of at most 0.0003.
Values sent between devices are 32-bit elements; how exact they have to be, the bound alone decides.
A program may use at most 64 MiB of HBM per device.

v0:
```python
import jax
import jax.numpy as jnp
from jax import lax
from jax.sharding import Mesh
from jax.sharding import PartitionSpec as P

GX = ("gx_0", "gx_1")
GY = ("gy_0", "gy_1")
GX_GY = ("gx_0", "gx_1", "gy_0", "gy_1")


def in_blocks(x, dim, size):
    before, after = (x.shape[:dim], x.shape[dim + 1 :])
    return jnp.moveaxis(x.reshape(*before, size, -1, *after), dim, 0)


def summed_on_arrival(x, axis, dim):
    parts = in_blocks(x, dim, lax.axis_size(axis))
    arrived = lax.all_to_all(parts, axis, split_axis=0, concat_axis=0, tiled=True)
    return arrived.sum(axis=0)


def sum_by_axis(x, axes, dim):
    far, near = axes
    own = summed_on_arrival(in_blocks(x, dim, lax.axis_size(far)), near, dim + 1)
    return jnp.sum(lax.all_to_all(own, far, 0, 0, tiled=True), axis=0)


def rows_for(lines, size):
    spare = -lines.shape[0] % size
    if not spare:
        return lines
    return jnp.concatenate([lines, jnp.zeros((spare, *lines.shape[1:]), lines.dtype)])


def sent_to_all(x, axis):
    copies = jnp.broadcast_to(x, (lax.axis_size(axis), *x.shape))
    return lax.all_to_all(copies, axis, split_axis=0, concat_axis=0, tiled=True)


def laid_out(parts, dim):
    parts = jnp.moveaxis(parts, 0, dim)
    dims = parts.shape
    return parts.reshape(*dims[:dim], dims[dim] * dims[dim + 1], *dims[dim + 2 :])


def whole_of(x, axes, dim):
    far, near = axes
    first = sent_to_all(x, far)
    parts = jnp.swapaxes(sent_to_all(first, near), 0, 1)
    return laid_out(parts.reshape(-1, *x.shape), dim)


def nested_sum(x, axes):
    own = sum_by_axis(rows_for(x, lax.axis_size(axes[0]) * lax.axis_size(axes[1])), axes, 0)
    whole = whole_of(own, axes, 0)
    return whole[: len(x)].reshape(x.shape)


def together(arrays, axis):
    flat, at, finished = (jnp.concatenate([a.reshape(-1) for a in arrays]), 0, [])
    total = nested_sum(flat, axis)
    for a in arrays:
        finished.append(total[at : at + a.size].reshape(a.shape))
        at += a.size
    return tuple(finished)


def total_of(x, axes):
    lines = x.reshape(-1)
    own = sum_by_axis(rows_for(lines, lax.axis_size(axes[0]) * lax.axis_size(axes[1])), axes, 0)
    whole = whole_of(own, axes, 0)
    return whole[: len(lines)].reshape(x.shape)


def fdot(left, right):
    return jnp.dot(left, right, precision=lax.Precision.HIGHEST, preferred_element_type=jnp.float32)


def normalize(block, gram):
    lower = jnp.linalg.cholesky(gram)
    return jax.scipy.linalg.solve_triangular(lower, block.T, lower=True).T


def per_device(trial, resid, energy, shift):
    count = trial.shape[0] * lax.axis_size(GX) * lax.axis_size(GY)
    corr = resid / (energy[:, None] - shift[None, :])
    local_first = fdot(trial.T, corr)
    raw_first, raw_metric = together(
        (local_first, fdot(trial.T, trial)), (("gx_0", "gx_1"), ("gy_0", "gy_1"))
    )
    coef_one = raw_first / count
    coef_two = (raw_first - fdot(raw_metric, coef_one)) / count
    work_two = corr - fdot(trial, coef_one + coef_two)
    gram_one = total_of(fdot(work_two.T, work_two), (("gx_0", "gx_1"), ("gy_0", "gy_1"))) / count
    return normalize(work_two, gram_one)


def solution(mesh):
    split = Mesh(mesh.devices.reshape(4, 2, 8, 8), ("gx_0", "gx_1", "gy_0", "gy_1"))
    in_specs = (P(GX_GY, None), P(GX_GY, None), P(GX_GY), P())
    out_specs = P(GX_GY, None)
    return jax.shard_map(
        per_device, mesh=split, in_specs=in_specs, out_specs=out_specs, check_vma=False
    )
```

profile of v0, /device:TPU:1, one launch (start us, length us, event | category | flops | bytes accessed | tf_op | source)
XLA Modules:
  0.0 187.2 jit_solution(17032278143547810166)
XLA Ops:
  0.0 0.0 copy-start
  0.0 1.5 copy.16
  1.6 0.3 copy-done
  1.9 0.0 copy-start.1
  1.9 0.0 copy-start.2
  1.9 0.0 copy-start.3
  1.9 4.7 %fusion.7 = f32[384,384]{1,0:T(8,128)} fusion(f32[1536,384]{1,0:T(8,128)S(1)} %copy-done), kind=kOutput, calls=%fused_computation.22 | convolution fusion | flops 2717908992 | bytes 2949120 | tf_op jit(solution)/shard_map/dot_general | solution.py:77
  6.6 0.0 copy-done.1
  6.6 0.0 copy-done.2
  6.6 0.0 copy-done.3
  6.6 1.8 convolution_bitcast_fusion.1
  8.4 0.1 copy.17
  8.5 1.9 %reshape.44 = f32[147456]{0:T(1024)} reshape(f32[384,384]{1,0:T(8,128)} %fusion.7) | data formatting | bytes 1179648 | tf_op jit(solution)/shard_map/reshape | solution.py:61
  10.5 1.1 pad_maximum_fusion
  11.6 1.1 reshape_reshape.4
  12.7 1.6 copy.18
  14.2 38.6 %all_to_all.56 = f32[64,8,384]{2,1,0:T(8,128)S(1)} all-to-all(f32[64,8,384]{2,1,0:T(8,128)S(1)} %copy.18), channel_id=1, replica_groups=mesh['gx_0'=4,'gx_1'=2,'gy_0'=8,'gy_1'=8] {'gy_0','gy_1'}, dimensions={0} | all-to-all | bytes 1572864 | tf_op jit(solution)/shard_map/all_to_all | solution.py:19
  52.9 0.1 reduce_sum.36
  53.0 11.5 %all_to_all.57 = f32[8,1,384]{2,1,0:T(1,128)S(1)} all-to-all(f32[8,1,384]{2,1,0:T(1,128)S(1)} %all_to_all.37), channel_id=1, replica_groups=mesh['gx_0'=4,'gx_1'=2,'gy_0'=8,'gy_1'=8] {'gx_0','gx_1'}, dimensions={0} | all-to-all | bytes 24576 | tf_op jit(solution)/shard_map/all_to_all | solution.py:26
  64.6 7.7 %all_to_all.58 = f32[8,1,384]{2,1,0:T(1,128)S(1)} all-to-all(f32[8,1,384]{2,1,0:T(1,128)S(1)} %broadcast_in_dim.16), channel_id=1, replica_groups=mesh['gx_0'=4,'gx_1'=2,'gy_0'=8,'gy_1'=8] {'gx_0','gx_1'}, dimensions={0} | all-to-all | bytes 24576 | tf_op jit(solution)/shard_map/all_to_all | solution.py:38
  72.3 0.1 broadcast_in_dim.17
  72.3 28.0 %all_to_all.59 = f32[64,8,384]{2,1,0:T(8,128)S(1)} all-to-all(f32[64,8,384]{2,1,0:T(8,128)S(1)} %broadcast_in_dim.17), channel_id=1, replica_groups=mesh['gx_0'=4,'gx_1'=2,'gy_0'=8,'gy_1'=8] {'gy_0','gy_1'}, dimensions={0} | all-to-all | bytes 1572864 | tf_op jit(solution)/shard_map/all_to_all | solution.py:38
  100.3 0.2 copy.26
  100.6 0.6 fusion.2
  101.3 3.7 %fusion = f32[1536,128]{0,1:T(8,128)S(1)} fusion(f32[384,128]{1,0:T(8,128)S(1)} %fusion.2, f32[1536,384]{1,0:T(8,128)S(1)} %copy-done, f32[1536,128]{0,1:T(8,128)} %copy-done.1, f32[128]{0:T(128)S(1)} %copy-done.3, f32[1536]{0:T(1024)S(1)} %copy-done.2), kind=kOutput, calls=%fused_computation.1 | convolution fusion | flops 906559488 | bytes 4135424 | tf_op jit(solution)/shard_map/dot_general | solution.py:77
  105.0 0.8 fusion.8
  105.8 0.1 reshape_reshape_reshape.4
  105.9 0.9 copy.20
  106.8 1.1 reshape.47
  107.9 19.4 %all_to_all.60 = f32[64,1,256]{2,1,0:T(1,128)S(1)} all-to-all(f32[64,1,256]{2,1,0:T(1,128)S(1)} %reshape.47), channel_id=1, replica_groups=mesh['gx_0'=4,'gx_1'=2,'gy_0'=8,'gy_1'=8] {'gy_0','gy_1'}, dimensions={0} | all-to-all | bytes 131072 | tf_op jit(solution)/shard_map/all_to_all | solution.py:19
  127.2 0.5 broadcast.78
  127.7 0.8 reduce.8
  128.5 0.1 reshape.48
  128.7 0.1 reduce_sum.38
  128.7 9.3 %all_to_all.61 = f32[8,1,32]{2,1,0:T(1,128)S(1)} all-to-all(f32[8,1,32]{2,1,0:T(1,128)S(1)} %bitcast.46), channel_id=1, replica_groups=mesh['gx_0'=4,'gx_1'=2,'gy_0'=8,'gy_1'=8] {'gx_0','gx_1'}, dimensions={0} | all-to-all | bytes 2048 | tf_op jit(solution)/shard_map/all_to_all | solution.py:26
  138.0 7.6 %all_to_all.62 = f32[8,1,32]{2,1,0:T(1,128)S(1)} all-to-all(f32[8,1,32]{2,1,0:T(1,128)S(1)} %broadcast_in_dim.18), channel_id=1, replica_groups=mesh['gx_0'=4,'gx_1'=2,'gy_0'=8,'gy_1'=8] {'gx_0','gx_1'}, dimensions={0} | all-to-all | bytes 2048 | tf_op jit(solution)/shard_map/all_to_all | solution.py:38
  145.7 0.2 reshape.49
  145.9 15.0 %all_to_all.63 = f32[64,1,256]{2,1,0:T(1,128)S(1)} all-to-all(f32[64,1,256]{2,1,0:T(1,128)S(1)} %reshape.49), channel_id=1, replica_groups=mesh['gx_0'=4,'gx_1'=2,'gy_0'=8,'gy_1'=8] {'gy_0','gy_1'}, dimensions={0} | all-to-all | bytes 131072 | tf_op jit(solution)/shard_map/all_to_all | solution.py:38
  160.8 0.8 reduce.9
  161.6 0.1 reshape.50
  161.8 0.1 copy.21
  161.8 0.1 div.39
  162.0 0.1 copy.22
  162.1 11.7 %cholesky.16 = f32[128,128]{1,0:T(8,128)S(1)} custom-call(f32[128,128]{1,0:T(8,128)S(1)} %fusion.6), custom_call_target="Cholesky" | custom-call | tf_op jit(solution)/shard_map/jit(cholesky)/cholesky | solution.py:81
  173.8 0.6 compare_reduce_fusion
  174.5 0.7 fusion.3
  175.1 9.8 %custom-call.7 = f32[1,128,128]{1,2,0:T(8,128)S(1)} custom-call(f32[1,128,128]{2,1,0:T(8,128)S(1)} %fusion.3), custom_call_target="InvertDiagBlocksLowerTriangular" | custom-call | tf_op jit(solution)/shard_map/jit(_solve_triangular)/triangular_solve | solution.py:82
  184.9 2.3 %fusion.4 = f32[1536,128]{1,0:T(8,128)} fusion(f32[1536,128]{0,1:T(8,128)S(1)} %fusion, f32[1,128,128]{1,2,0:T(8,128)S(1)} %custom-call.7), kind=kOutput, calls=%fused_computation.13 | convolution fusion | flops 301989888 | bytes 1638400 | tf_op jit(solution)/shard_map/jit(_solve_triangular)/triangular_solve | solution.py:82
  (14 shorter events, 0.3 us)
Async XLA Ops:
  0.0 1.9 %copy-start = (f32[1536,384]{1,0:T(8,128)S(1)}, f32[1536,384]{1,0:T(8,128)}, u32[]{:S(2)}) copy-start(f32[1536,384]{1,0:T(8,128)} %param.4) | copy-start | bytes 7077892
  1.9 4.7 %copy-start.1 = (f32[1536,128]{0,1:T(8,128)}, f32[1536,128]{0,1:T(8,128)S(1)}, u32[]{:S(2)}) copy-start(f32[1536,128]{0,1:T(8,128)S(1)} %copy.16) | copy-start | bytes 2359300
  1.9 4.7 %copy-start.2 = (f32[1536]{0:T(1024)S(1)}, f32[1536]{0:T(1024)}, u32[]{:S(2)}) copy-start(f32[1536]{0:T(1024)} %param.6) | copy-start | bytes 18436
  1.9 4.7 %copy-start.3 = (f32[128]{0:T(128)S(1)}, f32[128]{0:T(128)}, u32[]{:S(2)}) copy-start(f32[128]{0:T(128)} %param.7) | copy-start | bytes 1540
where the time goes:
time: 188 us; the launch traced here: 187 us
  blocking collectives  137 us (73%)
  other arithmetic  25.8 us (14%)
  matrix products  13.9 us (7%)
  local copies, waits for them, and re-layouts  10.1 us (5%)
    all_to_all x4, blocking collectives, sent_to_all(): return lax.all_to_all(copies, axis, split_axis=0, concat_axis=0, tiled=True)  58.3 us
    all_to_all x2, blocking collectives, summed_on_arrival(): lax.all_to_all(parts, axis, split_axis=0, concat_axis=0, tiled=True)  58 us
    all_to_all x2, blocking collectives, sum_by_axis(): return jnp.sum(lax.all_to_all(own, far, 0, 0, tiled=True), axis=0)  20.8 us
    another operation x3, other arithmetic, normalize(): lower = jnp.linalg.cholesky(gram)  12.4 us
    dot_general x5, matrix products, fdot(): jnp.dot(left, right, precision=lax.Precision.HIGHEST, preferred_element_t...  11.6 us
    another operation x2, other arithmetic, normalize(): return jax.scipy.linalg.solve_triangular(lower, block.T, lower=True).T  10.5 us

commit v1 on v0

v1 whole, which is shorter than its diff:
```python
import jax
import jax.numpy as jnp
from jax import lax
from jax.experimental import pallas as pl
from jax.experimental.pallas import tpu as pltpu
from jax.sharding import Mesh
from jax.sharding import PartitionSpec as P

MESH = pl.DeviceIdType.MESH
AXES = ("x", "core", "y", "z")
ROWS, KEEP, NEW = 1536, 384, 128
UNIT = 4
PAIRS = [(i, j) for i in range(4) for j in range(i, 4)]
HALF = len(PAIRS) * 128 // UNIT // 2
PLANE, LINE = 32, 8
CHUNK = HALF // PLANE
F32, BF16 = jnp.float32, jnp.bfloat16


def tdot(a, b):
    return lax.dot_general(a, b, (((0,), (0,)), ((), ())), preferred_element_type=F32)


def gram_kernel(
    trial_ref, resid_ref, energy_ref, shift_ref, total_ref, corr_ref,
    hi, lo, part, peer, held, own, line, done,
    core_sems, plane_sems, line_sems, gather_sems, spread_sems, last_sems,
):
    x, c = lax.axis_index("x"), lax.axis_index("core")
    y, z = lax.axis_index("y"), lax.axis_index("z")
    p = (1 - c) * y + c * z
    q = (1 - c) * z + c * y
    me = x * 8 + p
    other = {"x": x, "core": 1 - c, "y": y, "z": z}

    def in_plane(k):
        a, b = k // 8, k % 8
        return {"x": a, "core": c, "y": (1 - c) * b + c * y, "z": (1 - c) * z + c * b}

    def in_line(b):
        return {"x": x, "core": c, "y": (1 - c) * y + c * b, "z": (1 - c) * b + c * z}

    barrier = pltpu.get_barrier_semaphore()

    def greet_plane(j, _):
        pl.semaphore_signal(barrier, inc=1, device_id=in_plane((me + j) % PLANE), device_id_type=MESH)
        return _

    def greet_line(j, _):
        pl.semaphore_signal(barrier, inc=1, device_id=in_line((q + j) % LINE), device_id_type=MESH)
        return _

    pl.semaphore_signal(barrier, inc=1, device_id=other, device_id_type=MESH)
    lax.fori_loop(1, PLANE, greet_plane, 0)
    lax.fori_loop(1, LINE, greet_line, 0)

    shift = shift_ref[...]
    for b in range(ROWS // 128):
        rows = pl.ds(b * 128, 128)
        gap = jnp.broadcast_to(energy_ref[pl.ds(b, 1), :], (128, 128)).T - shift
        corr = resid_ref[rows, :] / gap
        corr_ref[rows, :] = corr
        trial = trial_ref[rows, :]
        high = trial.astype(BF16)
        hi[rows, :KEEP] = high
        lo[rows, :KEEP] = (trial - high.astype(F32)).astype(BF16)
        high = corr.astype(BF16)
        hi[rows, KEEP:] = high
        lo[rows, KEEP:] = (corr - high.astype(F32)).astype(BF16)

    cross = {}
    for i in range(2):
        left = hi[:, i * 256:(i + 1) * 256]
        for j in range(2):
            cross[i, j] = tdot(left, lo[:, j * 256:(j + 1) * 256])
    for i in range(2):
        left = hi[:, i * 256:(i + 1) * 256]
        for j in range(i, 2):
            full = tdot(left, hi[:, j * 256:(j + 1) * 256]) + cross[i, j] + cross[j, i].T
            for n, (s, t) in enumerate(PAIRS):
                if s // 2 == i and t // 2 == j:
                    block = full[s % 2 * 128:s % 2 * 128 + 128, t % 2 * 128:t % 2 * 128 + 128]
                    part[n * 32:(n + 1) * 32] = block.reshape(32, UNIT, 128)

    pl.semaphore_wait(barrier, PLANE + LINE - 1)

    def remote(src, dst, sems, device):
        return pltpu.make_async_remote_copy(
            src_ref=src, dst_ref=dst, send_sem=sems.at[0], recv_sem=sems.at[1],
            device_id=device, device_id_type=MESH,
        )

    mine, theirs = c * HALF, (1 - c) * HALF
    swap = remote(part.at[pl.ds(theirs, HALF)], peer, core_sems, other)
    swap.start()
    swap.wait_recv()
    peer[...] += part[pl.ds(mine, HALF)]

    def scatter(j, _):
        k = (me + j) % PLANE
        remote(
            peer.at[pl.ds(k * CHUNK, CHUNK)], held.at[pl.ds((j - 1) * CHUNK, CHUNK)], plane_sems, in_plane(k)
        ).start()
        return _

    lax.fori_loop(1, PLANE, scatter, 0)
    arrived = remote(held, held, plane_sems, other)
    arrived.wait_recv()
    total = peer[pl.ds(me * CHUNK, CHUNK)]
    for j in range(PLANE - 1):
        total += held[j * CHUNK:(j + 1) * CHUNK]
    own[...] = total
    line[pl.ds(q * CHUNK, CHUNK)] = total

    def exchange(j, _):
        remote(own, line.at[pl.ds(q * CHUNK, CHUNK)], line_sems, in_line((q + j) % LINE)).start()
        return _

    lax.fori_loop(1, LINE, exchange, 0)
    lines = line.at[pl.ds(0, (LINE - 1) * CHUNK)]
    remote(lines, lines, line_sems, other).wait_recv()
    total = line[0:CHUNK]
    for j in range(1, LINE):
        total += line[j * CHUNK:(j + 1) * CHUNK]
    done[...] = total
    total_ref[pl.ds(mine + me * CHUNK, CHUNK)] = total

    def chunk_of(k):
        return total_ref.at[pl.ds(mine + k * CHUNK, CHUNK)]

    def spread(j, _):
        k = (me + j) % PLANE
        pltpu.make_async_remote_copy(
            src_ref=done, dst_ref=chunk_of(me), send_sem=gather_sems.at[0], recv_sem=spread_sems.at[me],
            device_id=in_plane(k), device_id_type=MESH,
        ).start()
        return _

    lax.fori_loop(1, PLANE, spread, 0)
    remote(done, chunk_of(me), last_sems, other).start()

    def forward(j, _):
        k = (me + j) % PLANE
        pltpu.make_async_remote_copy(
            src_ref=done, dst_ref=chunk_of(k), send_sem=gather_sems.at[0], recv_sem=spread_sems.at[k],
            device_id=other, device_id_type=MESH,
        ).wait_recv()
        remote(chunk_of(k), chunk_of(k), last_sems, other).start()
        return _

    lax.fori_loop(1, PLANE, forward, 0)
    whole = total_ref.at[pl.ds(theirs, HALF)]
    remote(whole, whole, last_sems, other).wait_recv()

    swap.wait_send()
    arrived.wait_send()
    remote(lines, lines, line_sems, other).wait_send()
    remote(held, held, gather_sems, other).wait_send()
    remote(whole, whole, last_sems, other).wait_send()


def gram(trial, resid, energy, shift):
    vmem = pl.BlockSpec(memory_space=pltpu.VMEM)
    return pl.pallas_call(
        gram_kernel,
        out_shape=(
            jax.ShapeDtypeStruct((2 * HALF, UNIT, 128), F32),
            jax.ShapeDtypeStruct((ROWS, NEW), F32),
        ),
        in_specs=[vmem] * 4,
        out_specs=(vmem, vmem),
        scratch_shapes=[
            pltpu.VMEM((ROWS, KEEP + NEW), BF16),
            pltpu.VMEM((ROWS, KEEP + NEW), BF16),
            pltpu.VMEM((2 * HALF, UNIT, 128), F32),
            pltpu.VMEM((HALF, UNIT, 128), F32),
            pltpu.VMEM(((PLANE - 1) * CHUNK, UNIT, 128), F32),
            pltpu.VMEM((CHUNK, UNIT, 128), F32),
            pltpu.VMEM((LINE * CHUNK, UNIT, 128), F32),
            pltpu.VMEM((CHUNK, UNIT, 128), F32),
            pltpu.SemaphoreType.DMA((2,)),
            pltpu.SemaphoreType.DMA((2,)),
            pltpu.SemaphoreType.DMA((2,)),
            pltpu.SemaphoreType.DMA((2,)),
            pltpu.SemaphoreType.DMA((PLANE,)),
            pltpu.SemaphoreType.DMA((2,)),
        ],
        compiler_params=pltpu.CompilerParams(collective_id=0, has_side_effects=True),
        name="gram",
    )(trial, resid, energy.reshape(ROWS // 128, 128), shift.reshape(1, NEW))


def fdot(left, right):
    return jnp.dot(left, right, precision=lax.Precision.HIGHEST, preferred_element_type=F32)


def explicit(trial, resid, energy, shift, raw_first, raw_metric, count):
    corr = resid / (energy[:, None] - shift[None, :])
    def total(v):
        return lax.psum(v, AXES)
    work = corr
    for sweep in range(2):
        work = work - fdot(trial, total(fdot(trial.T, work)) / count)
    gram_two = total(fdot(work.T, work)) / count
    lower = jnp.linalg.cholesky(gram_two)
    return jax.scipy.linalg.solve_triangular(lower, work.T, lower=True).T


def per_device(trial, resid, energy, shift):
    count = ROWS * 512
    total, corr = gram(trial, resid, energy, shift)
    blocks = total.reshape(len(PAIRS), 128, 128) / count
    at = {pair: blocks[n] for n, pair in enumerate(PAIRS)}
    metric = jnp.concatenate(
        [jnp.concatenate([at[i, j] if i <= j else at[j, i].T for j in range(3)], 1) for i in range(3)], 0
    )
    first = jnp.concatenate([at[i, 3] for i in range(3)], 0)
    coef = 2 * first - fdot(metric, first)
    cross = fdot(coef.T, first)
    inner = fdot(coef.T, fdot(metric, coef))
    gram_one = at[3, 3] - cross - cross.T + inner
    terms = jnp.diagonal(at[3, 3]) + 2 * jnp.abs(jnp.diagonal(cross)) + jnp.diagonal(inner)
    steady = jnp.all(terms <= 16 * jnp.diagonal(gram_one))

    def fast():
        lower = jnp.linalg.cholesky(gram_one)
        inverse = jax.scipy.linalg.solve_triangular(lower, jnp.eye(NEW, dtype=F32), lower=True)
        return fdot(corr, inverse.T) - fdot(trial, fdot(coef, inverse.T))

    def slow():
        return explicit(trial, resid, energy, shift, None, None, count)

    return lax.cond(steady, fast, slow)


def solution(mesh):
    split = Mesh(mesh.devices.reshape(4, 2, 8, 8), AXES)
    in_specs = (P(AXES, None), P(AXES, None), P(AXES), P())
    return jax.shard_map(
        per_device, mesh=split, in_specs=in_specs, out_specs=P(AXES, None), check_vma=False
    )
```

time: 188 us -> 96.5 us (0.51)
  blocking collectives: 137 us -> 0 us
  Pallas kernels: 0 us -> 42.8 us
  between operations: 0.22 us -> 14.2 us
  matrix products: 13.9 us -> 7.38 us
  local copies, waits for them, and re-layouts: 10.1 us -> 6.85 us
    all_to_all x8 -> x0, blocking collectives: 137 us -> none  [the longest x4 58.3 us: sent_to_all(): return lax.all_to_all(copies, axis, split_axis=0, concat_axis=0, tiled=True)]
    pallas_call x0 -> x1, Pallas kernels: none -> 42.8 us  [gram(): pl.pallas_call(gram_kernel, out_shape=(jax.ShapeDtypeStruct((2 * HALF, UN...]
    gather x0 -> x4, local copies, waits for them, and re-layouts: none -> 5.02 us  [the longest x1 1.28 us: per_device(): steady = jnp.all(terms <= 16 * jnp.diagonal(gram_one))]
    dot_general x5 -> x7, matrix products: 11.6 us -> 7.13 us  [fdot(): jnp.dot(left, right, precision=lax.Precision.HIGHEST, preferred_element_t...]
    unnamed x14 -> x8, local copies, waits for them, and re-layouts: 3.38 us -> 0.9 us
    transpose x2, local copies, waits for them, and re-layouts: 2.45 us -> 0.19 us  [per_device(): at[j, i]]
    another operation x1, matrix products: 2.28 us -> 0.25 us  [fast(): jax.scipy.linalg.solve_triangular(lower, jnp.eye(NEW, dtype=F32), lower=T...]
    reshape x2 -> x0, local copies, waits for them, and re-layouts: 1.94 us -> none  [the longest x1 1.93 us: together(): a.reshape(-1)]
where the time goes in v1:
time: 96.5 us; the launch traced here: 96.3 us
  Pallas kernels  42.8 us (44%)
  other arithmetic  24.8 us (26%)
  between operations  14.2 us (15%)
  matrix products  7.38 us (8%)
  local copies, waits for them, and re-layouts  6.85 us (7%)
    pallas_call x1, Pallas kernels, gram(): pl.pallas_call(gram_kernel, out_shape=(jax.ShapeDtypeStruct((2 * HALF, UN...  42.8 us
    another operation x3, other arithmetic, fast(): lower = jnp.linalg.cholesky(gram_one)  12.4 us
    another operation x2, other arithmetic, fast(): jax.scipy.linalg.solve_triangular(lower, jnp.eye(NEW, dtype=F32), lower=T...  10.5 us
    dot_general x7, matrix products, fdot(): jnp.dot(left, right, precision=lax.Precision.HIGHEST, preferred_element_t...  7.13 us

profile of v1, /device:TPU:1, one launch (start us, length us, event | category | flops | bytes accessed | tf_op | source)
XLA Modules:
  0.0 96.3 jit_solution(4626774925823838280)
XLA Ops:
  6.5 42.8 %gram.1 = (f32[320,4,128]{2,1,0:T(4,128)}, f32[1536,128]{1,0:T(8,128)}) custom-call(f32[1536,384]{1,0:T(8,128)} %trial_ref.1, f32[1536,128]{1,0:T(8,128)} %resid_ref.1, f32[12,128]{1,0:T(8,128)} %bitcast.90, f32[1,128]{1,0:T(1,128)} %bitcast.99), custom_call_target="tpu_custom_call" | custom-call | tf_op jit(solution)/shard_map/gram/pallas_call | solution.py:164
  49.3 1.3 %broadcast_multiply_fusion.1 = f32[320,4,128]{2,1,0:T(4,128)S(1)} fusion(f32[320,4,128]{2,1,0:T(4,128)} %get-tuple-element.35), kind=kLoop, calls=%fused_computation.42 | loop fusion | flops 163840 | bytes 1310720 | tf_op jit(solution)/shard_map/div | solution.py:212
  50.6 1.2 %gather_fusion = f32[128]{0:T(128)S(1)} fusion(f32[128,128]{1,0:T(8,128)S(1)} %bitcast.73, s32[128]{0:T(128)S(1)} %or_bitcast_fusion), kind=kCustom, calls=%fused_computation | custom fusion | bytes 2048 | tf_op jit(solution)/shard_map/jit(diagonal)/cond/branch_0_fun/gather | solution.py:222
  51.9 0.1 copy.25
  52.0 0.1 copy.23
  52.1 0.1 copy.24
  52.2 0.1 copy.22
  52.3 0.6 convolution_subtract_fusion.1
  52.9 0.0 copy-start
  52.9 0.0 copy-start.3
  53.0 0.0 copy-start.4
  53.0 0.7 fusion.21
  53.6 0.5 fusion.17
  54.1 0.5 fusion.26
  54.6 1.2 %gather_fusion.2 = f32[128]{0:T(128)S(1)} fusion(f32[128,128]{1,0:T(8,128)S(1)} %fusion.26, s32[128]{0:T(128)S(1)} %or_bitcast_fusion), kind=kCustom, calls=%fused_computation.2 | custom fusion | bytes 2048 | tf_op jit(solution)/shard_map/jit(diagonal)/cond/branch_0_fun/gather | solution.py:222
  55.9 0.1 copy.27
  56.0 1.2 %gather_fusion.1 = f32[128]{0:T(128)S(1)} fusion(f32[128,128]{1,0:T(8,128)S(1)} %fusion.17, s32[128]{0:T(128)S(1)} %or_bitcast_fusion), kind=kCustom, calls=%fused_computation.1 | custom fusion | bytes 2048 | tf_op jit(solution)/shard_map/jit(diagonal)/cond/branch_0_fun/gather | solution.py:222
  57.2 0.1 copy.26
  57.3 1.3 %gather_fusion.3 = f32[128]{0:T(128)S(1)} fusion(f32[128,128]{0,1:T(8,128)S(1)} %fusion.18, s32[128]{0:T(128)S(1)} %or_bitcast_fusion), kind=kCustom, calls=%fused_computation.3 | custom fusion | bytes 2048 | tf_op jit(solution)/shard_map/jit(diagonal)/cond/branch_0_fun/gather | solution.py:223
  58.6 0.6 compare_reduce_fusion.2
  59.9 0.0 copy-done
  59.9 0.0 copy-done.3
  59.9 0.0 copy-done.4
  60.0 28.6 %conditional.1 = (f32[1536,128]{1,0:T(8,128)S(1)}) conditional(s32[]{:T(128)} %convert_element_type.4, (f32[1536]{0:T(1024)S(1)}, f32[128]{0:T(128)S(1)}, f32[1536,128]{1,0:T(8,128)}, f32[1536,384]{1,0:T(8,128)S(1)}) %tuple.41, (f32[128,128]{0,1:T(8,128)S(1)}, f32[1536,128]{1,0:T(8,128)}, f32[384,128]{1,0:T(8,128)S(1)}, ...), branch_computations={%region_1.0_spmd, %region_7.9_spmd} | conditional | flops 4229431552 | bytes 25573532 | solution.py:233
  60.2 0.1 copy.20
  60.3 11.7 %cholesky.55 = f32[128,128]{1,0:T(8,128)S(1)} custom-call(f32[128,128]{1,0:T(8,128)S(1)} %fusion.16), custom_call_target="Cholesky" | custom-call | tf_op jit(solution)/shard_map/cond/branch_1_fun/jit(cholesky)/cholesky | solution.py:226
  72.1 0.6 compare_reduce_fusion.1
  72.7 0.7 fusion.13
  73.4 9.8 %custom-call.9 = f32[1,128,128]{1,2,0:T(8,128)S(1)} custom-call(f32[1,128,128]{2,1,0:T(8,128)S(1)} %fusion.13), custom_call_target="InvertDiagBlocksLowerTriangular" | custom-call | tf_op jit(solution)/shard_map/cond/branch_1_fun/jit(_solve_triangular)/triangular_solve | solution.py:227
  83.2 0.2 fusion.14
  83.4 0.4 fusion.25
  83.8 1.9 %fusion.24 = f32[128,1536]{1,0:T(8,128)S(1)} fusion(f32[128,128]{1,0:T(8,128)S(1)} %fusion.14, f32[1536,128]{1,0:T(8,128)} %get-tuple-element.30), kind=kOutput, calls=%fused_computation.54 | convolution fusion | flops 301989888 | bytes 1638400 | tf_op jit(solution)/shard_map/cond/branch_1_fun/dot_general | solution.py:194
  85.7 2.6 %fusion.12 = f32[1536,128]{0,1:T(8,128)S(1)} fusion(f32[128,1536]{1,0:T(8,128)S(1)} %fusion.24, f32[128,384]{1,0:T(8,128)S(1)} %fusion.25, f32[1536,384]{1,0:T(8,128)S(1)} %get-tuple-element.32), kind=kOutput, calls=%fused_computation.29 | convolution fusion | flops 906166272 | bytes 4128768 | tf_op jit(solution)/shard_map/cond/branch_1_fun/dot_general | solution.py:194
  88.3 0.3 copy.21
  88.6 0.0 copy-start.2
  88.6 0.9 copy-done.2
  (5 shorter events, 0.1 us)
Async XLA Ops:
  52.9 7.0 %copy-start = (f32[1536,384]{1,0:T(8,128)S(1)}, f32[1536,384]{1,0:T(8,128)}, u32[]{:S(2)}) copy-start(f32[1536,384]{1,0:T(8,128)} %trial_ref.1) | copy-start | bytes 7077892
  52.9 7.0 %copy-start.3 = (f32[1536]{0:T(1024)S(1)}, f32[1536]{0:T(1024)}, u32[]{:S(2)}) copy-start(f32[1536]{0:T(1024)} %param.9) | copy-start | bytes 18436
  53.0 7.0 %copy-start.4 = (f32[128]{0:T(128)S(1)}, f32[128]{0:T(128)}, u32[]{:S(2)}) copy-start(f32[128]{0:T(128)} %param.10) | copy-start | bytes 1540
  88.6 0.9 copy-start.2

commit v2 on v1

--- a/solution.py
+++ b/solution.py
@@ -22,9 +22,9 @@
 
 
 def gram_kernel(
-    trial_ref, resid_ref, energy_ref, shift_ref, total_ref, corr_ref,
+    trial_ref, resid_ref, energy_ref, shift_ref, total_ref, high_ref, low_ref,
     hi, lo, part, peer, held, own, line, done,
-    core_sems, plane_sems, line_sems, gather_sems, spread_sems, last_sems,
+    core_sems, plane_sems, line_sems, gather_sems, spread_sems, last_sems, keep_sems,
 ):
     x, c = lax.axis_index("x"), lax.axis_index("core")
     y, z = lax.axis_index("y"), lax.axis_index("z")
@@ -59,7 +59,6 @@
         rows = pl.ds(b * 128, 128)
         gap = jnp.broadcast_to(energy_ref[pl.ds(b, 1), :], (128, 128)).T - shift
         corr = resid_ref[rows, :] / gap
-        corr_ref[rows, :] = corr
         trial = trial_ref[rows, :]
         high = trial.astype(BF16)
         hi[rows, :KEEP] = high
@@ -67,6 +66,13 @@
         high = corr.astype(BF16)
         hi[rows, KEEP:] = high
         lo[rows, KEEP:] = (corr - high.astype(F32)).astype(BF16)
+
+    keep = [
+        pltpu.make_async_copy(hi, high_ref, keep_sems.at[0]),
+        pltpu.make_async_copy(lo, low_ref, keep_sems.at[1]),
+    ]
+    for copy in keep:
+        copy.start()
 
     cross = {}
     for i in range(2):
@@ -152,6 +158,8 @@
     whole = total_ref.at[pl.ds(theirs, HALF)]
     remote(whole, whole, last_sems, other).wait_recv()
 
+    for copy in keep:
+        copy.wait()
     swap.wait_send()
     arrived.wait_send()
     remote(lines, lines, line_sems, other).wait_send()
@@ -161,14 +169,16 @@
 
 def gram(trial, resid, energy, shift):
     vmem = pl.BlockSpec(memory_space=pltpu.VMEM)
+    hbm = pl.BlockSpec(memory_space=pl.ANY)
     return pl.pallas_call(
         gram_kernel,
         out_shape=(
             jax.ShapeDtypeStruct((2 * HALF, UNIT, 128), F32),
-            jax.ShapeDtypeStruct((ROWS, NEW), F32),
+            jax.ShapeDtypeStruct((ROWS, KEEP + NEW), BF16),
+            jax.ShapeDtypeStruct((ROWS, KEEP + NEW), BF16),
         ),
         in_specs=[vmem] * 4,
-        out_specs=(vmem, vmem),
+        out_specs=(vmem, hbm, hbm),
         scratch_shapes=[
             pltpu.VMEM((ROWS, KEEP + NEW), BF16),
             pltpu.VMEM((ROWS, KEEP + NEW), BF16),
@@ -184,53 +194,203 @@
             pltpu.SemaphoreType.DMA((2,)),
             pltpu.SemaphoreType.DMA((PLANE,)),
             pltpu.SemaphoreType.DMA((2,)),
+            pltpu.SemaphoreType.DMA((2,)),
         ],
         compiler_params=pltpu.CompilerParams(collective_id=0, has_side_effects=True),
         name="gram",
     )(trial, resid, energy.reshape(ROWS // 128, 128), shift.reshape(1, NEW))
 
 
-def fdot(left, right):
-    return jnp.dot(left, right, precision=lax.Precision.HIGHEST, preferred_element_type=F32)
-
-
-def explicit(trial, resid, energy, shift, raw_first, raw_metric, count):
-    corr = resid / (energy[:, None] - shift[None, :])
-    def total(v):
-        return lax.psum(v, AXES)
-    work = corr
-    for sweep in range(2):
-        work = work - fdot(trial, total(fdot(trial.T, work)) / count)
-    gram_two = total(fdot(work.T, work)) / count
-    lower = jnp.linalg.cholesky(gram_two)
-    return jax.scipy.linalg.solve_triangular(lower, work.T, lower=True).T
-
-
-def per_device(trial, resid, energy, shift):
-    count = ROWS * 512
-    total, corr = gram(trial, resid, energy, shift)
-    blocks = total.reshape(len(PAIRS), 128, 128) / count
-    at = {pair: blocks[n] for n, pair in enumerate(PAIRS)}
+SIDE = 32
+
+
+def mul(left, right, dims):
+    return lax.dot_general(
+        left, right, ((dims[:1], dims[1:]), ((), ())), precision=lax.Precision.HIGHEST, preferred_element_type=F32
+    )
+
+
+def inverse_factor(square, lane, row):
+    tiles = SIDE // 8
+    sub = row[:8]
+    panels = []
+    rest = square
+    for base in range(0, NEW, SIDE):
+        here = (lane >= base) & (lane < base + SIDE)
+        top = rest[:SIDE]
+        cols = [
+            [jnp.broadcast_to(top[t * 8:t * 8 + 8, base + j:base + j + 1], (8, 128)) if t >= j // 8 else None
+             for t in range(tiles)]
+            for j in range(SIDE)
+        ]
+        unit = jnp.where(lane[:SIDE] == row[:SIDE] + base, 1.0, 0.0)
+        panel = jnp.where(here[:SIDE], unit, top)
+        panel = [panel[t * 8:t * 8 + 8] for t in range(tiles)]
+        for k in range(SIDE):
+            tk, sk = k // 8, k % 8
+            pivot = jnp.broadcast_to(cols[k][tk][sk:sk + 1], (8, 128))
+            scale = lax.rsqrt(pivot)
+            if k + 1 < SIDE:
+                tn, sn = (k + 1) // 8, (k + 1) % 8
+                line = jnp.broadcast_to(cols[k][tn][sn:sn + 1], (8, 128))
+                ratio = scale * scale
+                for t in range(tn, tiles):
+                    cols[k + 1][t] = cols[k + 1][t] - (cols[k][t] * line) * ratio
+            for t in range(tk, tiles):
+                cols[k][t] = cols[k][t] * scale
+            line = jnp.broadcast_to(panel[tk][sk:sk + 1], (8, 128)) * scale
+            panel[tk] = jnp.where(
+                sub == sk, line, panel[tk] - jnp.where(sub > sk, cols[k][tk], 0.0) * line
+            )
+            for t in range(tk + 1, tiles):
+                panel[t] = panel[t] - cols[k][t] * line
+            for j in range(k + 2, SIDE):
+                line = jnp.broadcast_to(cols[k][j // 8][j % 8:j % 8 + 1], (8, 128))
+                for t in range(j // 8, tiles):
+                    cols[j][t] = cols[j][t] - cols[k][t] * line
+        done = jnp.concatenate(panel, 0)
+        panels.append(done)
+        if base + SIDE < NEW:
+            left = rest.shape[0] - SIDE
+            below = jnp.where(here[:left], 0.0, rest[SIDE:])
+            rest = below - mul(done, done, (0, 0))[base + SIDE:]
+    whole = jnp.concatenate(panels, 0)
+    return jnp.where(lane <= row, whole, 0.0)
+
+
+def finish_kernel(count, total_ref, high_ref, low_ref, basis_ref, steady_ref, high, low, sems):
+    fetch = [
+        pltpu.make_async_copy(high_ref, high, sems.at[0]),
+        pltpu.make_async_copy(low_ref, low, sems.at[1]),
+    ]
+    for copy in fetch:
+        copy.start()
+    at = {
+        pair: total_ref[n * 32:(n + 1) * 32].reshape(128, 128) * (1.0 / count) for n, pair in enumerate(PAIRS)
+    }
     metric = jnp.concatenate(
         [jnp.concatenate([at[i, j] if i <= j else at[j, i].T for j in range(3)], 1) for i in range(3)], 0
     )
     first = jnp.concatenate([at[i, 3] for i in range(3)], 0)
-    coef = 2 * first - fdot(metric, first)
-    cross = fdot(coef.T, first)
-    inner = fdot(coef.T, fdot(metric, coef))
-    gram_one = at[3, 3] - cross - cross.T + inner
-    terms = jnp.diagonal(at[3, 3]) + 2 * jnp.abs(jnp.diagonal(cross)) + jnp.diagonal(inner)
-    steady = jnp.all(terms <= 16 * jnp.diagonal(gram_one))
-
-    def fast():
-        lower = jnp.linalg.cholesky(gram_one)
-        inverse = jax.scipy.linalg.solve_triangular(lower, jnp.eye(NEW, dtype=F32), lower=True)
-        return fdot(corr, inverse.T) - fdot(trial, fdot(coef, inverse.T))
-
-    def slow():
-        return explicit(trial, resid, energy, shift, None, None, count)
-
-    return lax.cond(steady, fast, slow)
+    second = mul(metric, first, (1, 0))
+    third = mul(metric, second, (1, 0))
+    coef = 2.0 * first - second
+    image = 2.0 * second - third
+    square = at[3, 3] + mul(coef, image - 2.0 * first, (0, 0))
+
+    lane = lax.broadcasted_iota(jnp.int32, (NEW, NEW), 1)
+    row = lax.broadcasted_iota(jnp.int32, (NEW, NEW), 0)
+    def on_diagonal(v):
+        return jnp.sum(jnp.where(lane == row, v, 0.0), axis=0, keepdims=True)
+    terms = on_diagonal(at[3, 3]) + jnp.sum(jnp.abs(coef) * (2.0 * jnp.abs(first) + jnp.abs(image)), axis=0, keepdims=True)
+    steady = jnp.where(terms <= 16.0 * on_diagonal(square), 1.0, 0.0)
+    steady_ref[...] = jnp.broadcast_to(jnp.min(steady, axis=1, keepdims=True), (8, 128))
+
+    inverse = inverse_factor(square, lane, row)
+    tail = jnp.concatenate([-mul(coef, inverse, (1, 1)), inverse.T], 0)
+    tail_high = tail.astype(BF16)
+    tail_low = (tail - tail_high.astype(F32)).astype(BF16)
+    both = jnp.concatenate([tail_high, tail_low], 1)
+    for copy in fetch:
+        copy.wait()
+
+    def rows_of(b, _):
+        rows = pl.ds(pl.multiple_of(b * 256, 256), 256)
+        two = jnp.dot(high[rows, :], both, preferred_element_type=F32)
+        one = jnp.dot(low[rows, :], tail_high, preferred_element_type=F32)
+        basis_ref[rows, :] = two[:, :128] + (two[:, 128:] + one)
+        return _
+
+    lax.fori_loop(0, ROWS // 256, rows_of, 0)
+
+
+def finish(total, high, low, count):
+    vmem = pl.BlockSpec(memory_space=pltpu.VMEM)
+    hbm = pl.BlockSpec(memory_space=pl.ANY)
+    return pl.pallas_call(
+        lambda *refs: finish_kernel(count, *refs),
+        out_shape=(jax.ShapeDtypeStruct((ROWS, NEW), F32), jax.ShapeDtypeStruct((8, 128), F32)),
+        in_specs=[vmem, hbm, hbm],
+        out_specs=(vmem, vmem),
+        scratch_shapes=[
+            pltpu.VMEM((ROWS, KEEP + NEW), BF16),
+            pltpu.VMEM((ROWS, KEEP + NEW), BF16),
+            pltpu.SemaphoreType.DMA((2,)),
+        ],
+        name="finish",
+    )(total, high, low)
+
+
+def in_blocks(x, dim, size):
+    before, after = (x.shape[:dim], x.shape[dim + 1 :])
+    return jnp.moveaxis(x.reshape(*before, size, -1, *after), dim, 0)
+
+
+def summed_on_arrival(x, axis, dim):
+    parts = in_blocks(x, dim, lax.axis_size(axis))
+    arrived = lax.all_to_all(parts, axis, split_axis=0, concat_axis=0, tiled=True)
+    return arrived.sum(axis=0)
+
+
+def sum_by_axis(x, axes, dim):
+    far, near = axes
+    own = summed_on_arrival(in_blocks(x, dim, lax.axis_size(far)), near, dim + 1)
+    return jnp.sum(lax.all_to_all(own, far, 0, 0, tiled=True), axis=0)
+
+
+def rows_for(lines, size):
+    spare = -lines.shape[0] % size
+    if not spare:
+        return lines
+    return jnp.concatenate([lines, jnp.zeros((spare, *lines.shape[1:]), lines.dtype)])
+
+
+def sent_to_all(x, axis):
+    copies = jnp.broadcast_to(x, (lax.axis_size(axis), *x.shape))
+    return lax.all_to_all(copies, axis, split_axis=0, concat_axis=0, tiled=True)
+
+
+def laid_out(parts, dim):
+    parts = jnp.moveaxis(parts, 0, dim)
+    dims = parts.shape
+    return parts.reshape(*dims[:dim], dims[dim] * dims[dim + 1], *dims[dim + 2 :])
+
+
+def whole_of(x, axes, dim):
+    far, near = axes
+    first = sent_to_all(x, far)
+    parts = jnp.swapaxes(sent_to_all(first, near), 0, 1)
+    return laid_out(parts.reshape(-1, *x.shape), dim)
+
+
+def nested_sum(x, axes):
+    own = sum_by_axis(rows_for(x, lax.axis_size(axes[0]) * lax.axis_size(axes[1])), axes, 0)
+    whole = whole_of(own, axes, 0)
+    return whole[: len(x)].reshape(x.shape)
+
+
+def fdot(left, right):
+    return jnp.dot(left, right, precision=lax.Precision.HIGHEST, preferred_element_type=F32)
+
+
+def explicit(trial, resid, energy, shift, count):
+    def total(v):
+        return nested_sum(v.reshape(-1), (("x", "core"), ("y", "z"))).reshape(v.shape)
+
+    work = resid / (energy[:, None] - shift[None, :])
+    for sweep in range(2):
+        work = work - fdot(trial, total(fdot(trial.T, work)) / count)
+    lower = jnp.linalg.cholesky(total(fdot(work.T, work)) / count)
+    return jax.scipy.linalg.solve_triangular(lower, work.T, lower=True).T
+
+
+def per_device(trial, resid, energy, shift):
+    count = ROWS * 512
+    total, high, low = gram(trial, resid, energy, shift)
+    basis, steady = finish(total, high, low, count)
+    return lax.cond(
+        steady[0, 0] > 0.5, lambda: basis, lambda: explicit(trial, resid, energy, shift, count)
+    )
 
 
 def solution(mesh):

time: 96.5 us -> 54.8 us (0.57)
  other arithmetic: 24.8 us -> 0 us
  between operations: 14.2 us -> 0.94 us
  Pallas kernels: 42.8 us -> 52.2 us
  matrix products: 7.38 us -> 0 us
  local copies, waits for them, and re-layouts: 6.85 us -> 1.29 us
    another operation x5 -> x0, other arithmetic: 22.9 us -> none  [the longest x3 12.4 us: fast(): lower = jnp.linalg.cholesky(gram_one)]
    pallas_call x0 -> x1, Pallas kernels: none -> 9.66 us  [finish(): pl.pallas_call(lambda *refs: finish_kernel(count, *refs), out_shape=(jax....]
    dot_general x7 -> x0, matrix products: 7.13 us -> none  [fdot(): jnp.dot(left, right, precision=lax.Precision.HIGHEST, preferred_element_t...]
    gather x4 -> x0, local copies, waits for them, and re-layouts: 5.02 us -> none  [the longest x1 1.28 us: per_device(): steady = jnp.all(terms <= 16 * jnp.diagonal(gram_one))]
    div x2 -> x0, other arithmetic: 1.27 us -> none  [the longest x1 1.26 us: per_device(): blocks = total.reshape(len(PAIRS), 128, 128) / count]
    slice x1, local copies, waits for them, and re-layouts: 0.05 us -> 1.27 us  [per_device(): steady[0, 0] > 0.5]
where the time goes in v2:
time: 54.8 us; the launch traced here: 54.6 us
  Pallas kernels  52.2 us (95%)
  local copies, waits for them, and re-layouts  1.29 us (2%)
  between operations  0.94 us (2%)
    pallas_call x1, Pallas kernels, gram(): pl.pallas_call(gram_kernel, out_shape=(jax.ShapeDtypeStruct((2 * HALF, UN...  42.5 us
    pallas_call x1, Pallas kernels, finish(): pl.pallas_call(lambda *refs: finish_kernel(count, *refs), out_shape=(jax....  9.66 us
    slice x1, local copies, waits for them, and re-layouts, per_device(): steady[0, 0] > 0.5  1.27 us

profile of v2, /device:TPU:1, one launch (start us, length us, event | category | flops | bytes accessed | tf_op | source)
XLA Modules:
  0.0 54.6 jit_solution(99591207171318675)
XLA Ops:
  0.0 42.5 %gram.1 = (f32[320,4,128]{2,1,0:T(4,128)}, bf16[1536,512]{1,0:T(8,128)(2,1)}, bf16[1536,512]{1,0:T(8,128)(2,1)}) custom-call(f32[1536,384]{1,0:T(8,128)} %trial_ref.1, f32[1536,128]{1,0:T(8,128)} %resid_ref.1, f32[12,128]{1,0:T(8,128)} %bitcast.52, f32[1,128]{1,0:T(1,128)} %bitcast.59), custom_call_target="tpu_custom_call" | custom-call | tf_op jit(solution)/shard_map/gram/pallas_call | solution.py:173
  42.5 0.0 copy-start
  42.5 0.0 copy-start.2
  42.5 0.0 copy-start.3
  42.5 9.7 %finish.1 = (f32[1536,128]{1,0:T(8,128)}, f32[8,128]{1,0:T(8,128)}) custom-call(f32[320,4,128]{2,1,0:T(4,128)} %get-tuple-element.26.refs_0_, bf16[1536,512]{1,0:T(8,128)(2,1)} %get-tuple-element.27.refs_1_, bf16[1536,512]{1,0:T(8,128)(2,1)} %get-tuple-element.28.refs_2_), custom_call_target="tpu_custom_call" | custom-call | tf_op jit(solution)/shard_map/finish/pallas_call | solution.py:310
  52.2 1.3 %slice.15 = f32[1,1]{1,0:T(1,128)} slice(f32[8,128]{1,0:T(8,128)} %get-tuple-element.29), slice={[0:1], [0:1]} | slice | bytes 8 | tf_op jit(solution)/shard_map/slice | solution.py:392
  54.2 0.0 copy-done
  54.2 0.0 copy-done.2
  54.2 0.0 copy-done.3
  54.2 0.2 conditional.1
Async XLA Ops:
  42.5 11.7 %copy-start = (f32[1536,384]{1,0:T(8,128)S(1)}, f32[1536,384]{1,0:T(8,128)}, u32[]{:S(2)}) copy-start(f32[1536,384]{1,0:T(8,128)} %trial_ref.1) | copy-start | bytes 7077892
  42.5 11.7 %copy-start.2 = (f32[1536]{0:T(1024)S(1)}, f32[1536]{0:T(1024)}, u32[]{:S(2)}) copy-start(f32[1536]{0:T(1024)} %param.8) | copy-start | bytes 18436
  42.5 11.7 %copy-start.3 = (f32[128]{0:T(128)S(1)}, f32[128]{0:T(128)}, u32[]{:S(2)}) copy-start(f32[128]{0:T(128)} %param.9) | copy-start | bytes 1540

commit v3 on v2

--- a/solution.py
+++ b/solution.py
@@ -9,11 +9,14 @@
 MESH = pl.DeviceIdType.MESH
 AXES = ("x", "core", "y", "z")
 ROWS, KEEP, NEW = 1536, 384, 128
+STEP = 384
 UNIT = 4
-PAIRS = [(i, j) for i in range(4) for j in range(i, 4)]
+PAIRS = [(0, 0), (0, 1), (1, 1), (0, 2), (0, 3), (2, 2), (2, 3), (3, 3), (1, 2), (1, 3)]
 HALF = len(PAIRS) * 128 // UNIT // 2
 PLANE, LINE = 32, 8
 CHUNK = HALF // PLANE
+NEAR = [(i, j) for i in range(4) for j in range(8) if (i, j) != (0, 0)]
+FAR = sorted(NEAR, key=lambda o: -min(o[0], 4 - o[0]) - min(o[1], 8 - o[1]))
 F32, BF16 = jnp.float32, jnp.bfloat16
 
 
@@ -23,49 +26,50 @@
 
 def gram_kernel(
     trial_ref, resid_ref, energy_ref, shift_ref, total_ref, high_ref, low_ref,
-    hi, lo, part, peer, held, own, line, done,
-    core_sems, plane_sems, line_sems, gather_sems, spread_sems, last_sems, keep_sems,
+    trial, resid, energy, shift, hi, lo, part, peer, held, own, line, done,
+    load_sems, core_sems, plane_sems, line_sems, gather_sems, spread_sems, last_sems, keep_sems,
 ):
+    loads = [
+        pltpu.make_async_copy(energy_ref, energy, load_sems.at[0]),
+        pltpu.make_async_copy(shift_ref, shift, load_sems.at[1]),
+    ]
+    for b in range(ROWS // STEP):
+        rows = pl.ds(b * STEP, STEP)
+        loads.append(pltpu.make_async_copy(resid_ref.at[rows], resid.at[rows], load_sems.at[2 + 2 * b]))
+        loads.append(pltpu.make_async_copy(trial_ref.at[rows], trial.at[rows], load_sems.at[3 + 2 * b]))
+    for load in loads:
+        load.start()
+
     x, c = lax.axis_index("x"), lax.axis_index("core")
     y, z = lax.axis_index("y"), lax.axis_index("z")
     p = (1 - c) * y + c * z
     q = (1 - c) * z + c * y
     me = x * 8 + p
     other = {"x": x, "core": 1 - c, "y": y, "z": z}
-
-    def in_plane(k):
-        a, b = k // 8, k % 8
-        return {"x": a, "core": c, "y": (1 - c) * b + c * y, "z": (1 - c) * z + c * b}
-
-    def in_line(b):
-        return {"x": x, "core": c, "y": (1 - c) * y + c * b, "z": (1 - c) * b + c * z}
+    xs = [(x + i) % 4 for i in range(4)]
+    ps = [(p + j) % 8 for j in range(8)]
+    qs = [(q + j) % 8 for j in range(8)]
+
+    def in_plane(i, j):
+        return {"x": xs[i], "core": c, "y": (1 - c) * ps[j] + c * y, "z": (1 - c) * z + c * ps[j]}
+
+    def in_line(j):
+        return {"x": x, "core": c, "y": (1 - c) * y + c * qs[j], "z": (1 - c) * qs[j] + c * z}
 
     barrier = pltpu.get_barrier_semaphore()
-
-    def greet_plane(j, _):
-        pl.semaphore_signal(barrier, inc=1, device_id=in_plane((me + j) % PLANE), device_id_type=MESH)
-        return _
-
-    def greet_line(j, _):
-        pl.semaphore_signal(barrier, inc=1, device_id=in_line((q + j) % LINE), device_id_type=MESH)
-        return _
-
-    pl.semaphore_signal(barrier, inc=1, device_id=other, device_id_type=MESH)
-    lax.fori_loop(1, PLANE, greet_plane, 0)
-    lax.fori_loop(1, LINE, greet_line, 0)
-
-    shift = shift_ref[...]
-    for b in range(ROWS // 128):
-        rows = pl.ds(b * 128, 128)
-        gap = jnp.broadcast_to(energy_ref[pl.ds(b, 1), :], (128, 128)).T - shift
-        corr = resid_ref[rows, :] / gap
-        trial = trial_ref[rows, :]
-        high = trial.astype(BF16)
-        hi[rows, :KEEP] = high
-        lo[rows, :KEEP] = (trial - high.astype(F32)).astype(BF16)
-        high = corr.astype(BF16)
-        hi[rows, KEEP:] = high
-        lo[rows, KEEP:] = (corr - high.astype(F32)).astype(BF16)
+    for device in [other] + [in_plane(i, j) for i, j in FAR] + [in_line(j) for j in range(1, 8)]:
+        pl.semaphore_signal(barrier, inc=1, device_id=device, device_id_type=MESH)
+
+    for b in range(ROWS // STEP):
+        for load in loads[2 * b + 2:2 * b + 4] + (loads[:2] if b == 0 else []):
+            load.wait()
+        for r in range(b * STEP, (b + 1) * STEP, 128):
+            rows = pl.ds(r, 128)
+            gap = jnp.broadcast_to(energy[pl.ds(r // 128, 1), :], (128, 128)).T - shift[...]
+            for at, value in ((slice(0, KEEP), trial[rows, :]), (slice(KEEP, KEEP + NEW), resid[rows, :] / gap)):
+                high = value.astype(BF16)
+                hi[rows, at] = high
+                lo[rows, at] = (value - high.astype(F32)).astype(BF16)
 
     keep = [
         pltpu.make_async_copy(hi, high_ref, keep_sems.at[0]),
@@ -74,21 +78,17 @@
     for copy in keep:
         copy.start()
 
-    cross = {}
-    for i in range(2):
-        left = hi[:, i * 256:(i + 1) * 256]
-        for j in range(2):
-            cross[i, j] = tdot(left, lo[:, j * 256:(j + 1) * 256])
-    for i in range(2):
-        left = hi[:, i * 256:(i + 1) * 256]
-        for j in range(i, 2):
-            full = tdot(left, hi[:, j * 256:(j + 1) * 256]) + cross[i, j] + cross[j, i].T
-            for n, (s, t) in enumerate(PAIRS):
-                if s // 2 == i and t // 2 == j:
-                    block = full[s % 2 * 128:s % 2 * 128 + 128, t % 2 * 128:t % 2 * 128 + 128]
-                    part[n * 32:(n + 1) * 32] = block.reshape(32, UNIT, 128)
-
-    pl.semaphore_wait(barrier, PLANE + LINE - 1)
+    def half(h):
+        wide = pl.ds(pl.multiple_of(h * 256, 256), 256)
+        thin = pl.ds(pl.multiple_of(h * 128, 128), 128)
+        left = hi[:, wide]
+        cross = tdot(left, lo[:, wide])
+        full = tdot(left, left) + (cross + cross.T)
+        left = hi[:, thin]
+        side = tdot(left, hi[:, 256:]) + (tdot(left, lo[:, 256:]) + tdot(lo[:, thin], hi[:, 256:]))
+        blocks = (full[:128, :128], full[:128, 128:], full[128:, 128:], side[:, :128], side[:, 128:])
+        for n, block in enumerate(blocks):
+            part[pl.ds(h * HALF + n * 32, 32)] = block.reshape(32, UNIT, 128)
 
     def remote(src, dst, sems, device):
         return pltpu.make_async_remote_copy(
@@ -97,19 +97,19 @@
         )
 
     mine, theirs = c * HALF, (1 - c) * HALF
+    half(1 - c)
+    pl.semaphore_wait(barrier, PLANE + LINE - 1)
     swap = remote(part.at[pl.ds(theirs, HALF)], peer, core_sems, other)
     swap.start()
+    half(c)
     swap.wait_recv()
     peer[...] += part[pl.ds(mine, HALF)]
 
-    def scatter(j, _):
-        k = (me + j) % PLANE
+    for n, (i, j) in enumerate(FAR):
+        k = xs[i] * 8 + ps[j]
         remote(
-            peer.at[pl.ds(k * CHUNK, CHUNK)], held.at[pl.ds((j - 1) * CHUNK, CHUNK)], plane_sems, in_plane(k)
+            peer.at[pl.ds(k * CHUNK, CHUNK)], held.at[pl.ds(n * CHUNK, CHUNK)], plane_sems, in_plane(i, j)
         ).start()
-        return _
-
-    lax.fori_loop(1, PLANE, scatter, 0)
     arrived = remote(held, held, plane_sems, other)
     arrived.wait_recv()
     total = peer[pl.ds(me * CHUNK, CHUNK)]
@@ -118,11 +118,8 @@
     own[...] = total
     line[pl.ds(q * CHUNK, CHUNK)] = total
 
-    def exchange(j, _):
-        remote(own, line.at[pl.ds(q * CHUNK, CHUNK)], line_sems, in_line((q + j) % LINE)).start()
-        return _
-
-    lax.fori_loop(1, LINE, exchange, 0)
+    for j in (4, 3, 5, 2, 6, 1, 7):
+        remote(own, line.at[pl.ds(q * CHUNK, CHUNK)], line_sems, in_line(j)).start()
     lines = line.at[pl.ds(0, (LINE - 1) * CHUNK)]
     remote(lines, lines, line_sems, other).wait_recv()
     total = line[0:CHUNK]
@@ -134,27 +131,19 @@
     def chunk_of(k):
         return total_ref.at[pl.ds(mine + k * CHUNK, CHUNK)]
 
-    def spread(j, _):
-        k = (me + j) % PLANE
-        pltpu.make_async_remote_copy(
-            src_ref=done, dst_ref=chunk_of(me), send_sem=gather_sems.at[0], recv_sem=spread_sems.at[me],
-            device_id=in_plane(k), device_id_type=MESH,
-        ).start()
-        return _
-
-    lax.fori_loop(1, PLANE, spread, 0)
+    def spread(n, k, device):
+        return pltpu.make_async_remote_copy(
+            src_ref=done, dst_ref=chunk_of(k), send_sem=gather_sems.at[0], recv_sem=spread_sems.at[n],
+            device_id=device, device_id_type=MESH,
+        )
+
+    for n, (i, j) in enumerate(NEAR):
+        spread(n, me, in_plane(i, j)).start()
     remote(done, chunk_of(me), last_sems, other).start()
-
-    def forward(j, _):
-        k = (me + j) % PLANE
-        pltpu.make_async_remote_copy(
-            src_ref=done, dst_ref=chunk_of(k), send_sem=gather_sems.at[0], recv_sem=spread_sems.at[k],
-            device_id=other, device_id_type=MESH,
-        ).wait_recv()
+    for n, (i, j) in enumerate(NEAR):
+        k = xs[-i % 4] * 8 + ps[-j % 8]
+        spread(n, k, other).wait_recv()
         remote(chunk_of(k), chunk_of(k), last_sems, other).start()
-        return _
-
-    lax.fori_loop(1, PLANE, forward, 0)
     whole = total_ref.at[pl.ds(theirs, HALF)]
     remote(whole, whole, last_sems, other).wait_recv()
 
@@ -177,9 +166,13 @@
             jax.ShapeDtypeStruct((ROWS, KEEP + NEW), BF16),
             jax.ShapeDtypeStruct((ROWS, KEEP + NEW), BF16),
         ),
-        in_specs=[vmem] * 4,
+        in_specs=[hbm] * 4,
         out_specs=(vmem, hbm, hbm),
         scratch_shapes=[
+            pltpu.VMEM((ROWS, KEEP), F32),
+            pltpu.VMEM((ROWS, NEW), F32),
+            pltpu.VMEM((ROWS // 128, 128), F32),
+            pltpu.VMEM((1, NEW), F32),
             pltpu.VMEM((ROWS, KEEP + NEW), BF16),
             pltpu.VMEM((ROWS, KEEP + NEW), BF16),
             pltpu.VMEM((2 * HALF, UNIT, 128), F32),
@@ -188,6 +181,7 @@
             pltpu.VMEM((CHUNK, UNIT, 128), F32),
             pltpu.VMEM((LINE * CHUNK, UNIT, 128), F32),
             pltpu.VMEM((CHUNK, UNIT, 128), F32),
+            pltpu.SemaphoreType.DMA((2 + 2 * ROWS // STEP,)),
             pltpu.SemaphoreType.DMA((2,)),
             pltpu.SemaphoreType.DMA((2,)),
             pltpu.SemaphoreType.DMA((2,)),
@@ -284,7 +278,7 @@
         return jnp.sum(jnp.where(lane == row, v, 0.0), axis=0, keepdims=True)
     terms = on_diagonal(at[3, 3]) + jnp.sum(jnp.abs(coef) * (2.0 * jnp.abs(first) + jnp.abs(image)), axis=0, keepdims=True)
     steady = jnp.where(terms <= 16.0 * on_diagonal(square), 1.0, 0.0)
-    steady_ref[...] = jnp.broadcast_to(jnp.min(steady, axis=1, keepdims=True), (8, 128))
+    steady_ref[0, 0] = jnp.min(steady)
 
     inverse = inverse_factor(square, lane, row)
     tail = jnp.concatenate([-mul(coef, inverse, (1, 1)), inverse.T], 0)
@@ -309,9 +303,9 @@
     hbm = pl.BlockSpec(memory_space=pl.ANY)
     return pl.pallas_call(
         lambda *refs: finish_kernel(count, *refs),
-        out_shape=(jax.ShapeDtypeStruct((ROWS, NEW), F32), jax.ShapeDtypeStruct((8, 128), F32)),
+        out_shape=(jax.ShapeDtypeStruct((ROWS, NEW), F32), jax.ShapeDtypeStruct((1, 1), F32)),
         in_specs=[vmem, hbm, hbm],
-        out_specs=(vmem, vmem),
+        out_specs=(vmem, pl.BlockSpec(memory_space=pltpu.SMEM)),
         scratch_shapes=[
             pltpu.VMEM((ROWS, KEEP + NEW), BF16),
             pltpu.VMEM((ROWS, KEEP + NEW), BF16),

time: 54.8 us -> 50.7 us (0.925)
  Pallas kernels: 52.2 us -> 49.4 us
  local copies, waits for them, and re-layouts: 1.29 us -> 0.02 us
    pallas_call x1, Pallas kernels: 42.5 us -> 39.7 us  [gram(): pl.pallas_call(gram_kernel, out_shape=(jax.ShapeDtypeStruct((2 * HALF, UN...]
    slice x1 -> x0, local copies, waits for them, and re-layouts: 1.27 us -> none  [per_device(): steady[0, 0] > 0.5]
where the time goes in v3:
time: 50.7 us; the launch traced here: 50.6 us
  Pallas kernels  49.4 us (97%)
  between operations  0.86 us (2%)
    pallas_call x1, Pallas kernels, gram(): pl.pallas_call(gram_kernel, out_shape=(jax.ShapeDtypeStruct((2 * HALF, UN...  39.7 us
    pallas_call x1, Pallas kernels, finish(): pl.pallas_call(lambda *refs: finish_kernel(count, *refs), out_shape=(jax....  9.75 us

profile of v3, /device:TPU:1, one launch (start us, length us, event | category | flops | bytes accessed | tf_op | source)
XLA Modules:
  0.0 50.6 jit_solution(12002918303832253950)
XLA Ops:
  0.0 39.7 %gram.1 = (f32[320,4,128]{2,1,0:T(4,128)}, bf16[1536,512]{1,0:T(8,128)(2,1)}, bf16[1536,512]{1,0:T(8,128)(2,1)}) custom-call(f32[1536,384]{1,0:T(8,128)} %trial_ref.1, f32[1536,128]{1,0:T(8,128)} %resid_ref.1, f32[12,128]{1,0:T(8,128)} %bitcast.52, f32[1,128]{1,0:T(1,128)} %bitcast.59), custom_call_target="tpu_custom_call" | custom-call | tf_op jit(solution)/shard_map/gram/pallas_call | solution.py:162
  39.7 0.0 copy-start
  39.7 0.0 copy-start.2
  39.7 0.0 copy-start.3
  39.7 9.7 %finish.1 = (f32[1536,128]{1,0:T(8,128)}, f32[1,1]{1,0:T(1,128)}) custom-call(f32[320,4,128]{2,1,0:T(4,128)} %get-tuple-element.26.refs_0_, bf16[1536,512]{1,0:T(8,128)(2,1)} %get-tuple-element.27.refs_1_, bf16[1536,512]{1,0:T(8,128)(2,1)} %get-tuple-element.28.refs_2_), custom_call_target="tpu_custom_call" | custom-call | tf_op jit(solution)/shard_map/finish/pallas_call | solution.py:304
  50.1 0.0 copy-done
  50.1 0.0 copy-done.2
  50.1 0.0 copy-done.3
  50.1 0.2 conditional.1
Async XLA Ops:
  39.7 10.4 %copy-start = (f32[1536,384]{1,0:T(8,128)S(1)}, f32[1536,384]{1,0:T(8,128)}, u32[]{:S(2)}) copy-start(f32[1536,384]{1,0:T(8,128)} %trial_ref.1) | copy-start | bytes 7077892
  39.7 10.4 %copy-start.2 = (f32[1536]{0:T(1024)S(1)}, f32[1536]{0:T(1024)}, u32[]{:S(2)}) copy-start(f32[1536]{0:T(1024)} %param.8) | copy-start | bytes 18436
  39.7 10.4 %copy-start.3 = (f32[128]{0:T(128)S(1)}, f32[128]{0:T(128)}, u32[]{:S(2)}) copy-start(f32[128]{0:T(128)} %param.9) | copy-start | bytes 1540

commit v4 on v3

--- a/solution.py
+++ b/solution.py
@@ -10,6 +10,7 @@
 AXES = ("x", "core", "y", "z")
 ROWS, KEEP, NEW = 1536, 384, 128
 STEP = 384
+VMEM_LIMIT = 24 * 2**20
 UNIT = 4
 PAIRS = [(0, 0), (0, 1), (1, 1), (0, 2), (0, 3), (2, 2), (2, 3), (3, 3), (1, 2), (1, 3)]
 HALF = len(PAIRS) * 128 // UNIT // 2
@@ -25,9 +26,9 @@
 
 
 def gram_kernel(
-    trial_ref, resid_ref, energy_ref, shift_ref, total_ref, high_ref, low_ref,
-    trial, resid, energy, shift, hi, lo, part, peer, held, own, line, done,
-    load_sems, core_sems, plane_sems, line_sems, gather_sems, spread_sems, last_sems, keep_sems,
+    trial_ref, resid_ref, energy_ref, shift_ref, total_ref, hi, lo,
+    trial, resid, energy, shift, part, peer, held, own, line, done,
+    load_sems, core_sems, plane_sems, line_sems, gather_sems, spread_sems, last_sems,
 ):
     loads = [
         pltpu.make_async_copy(energy_ref, energy, load_sems.at[0]),
@@ -70,13 +71,6 @@
                 high = value.astype(BF16)
                 hi[rows, at] = high
                 lo[rows, at] = (value - high.astype(F32)).astype(BF16)
-
-    keep = [
-        pltpu.make_async_copy(hi, high_ref, keep_sems.at[0]),
-        pltpu.make_async_copy(lo, low_ref, keep_sems.at[1]),
-    ]
-    for copy in keep:
-        copy.start()
 
     def half(h):
         wide = pl.ds(pl.multiple_of(h * 256, 256), 256)
@@ -147,8 +141,6 @@
     whole = total_ref.at[pl.ds(theirs, HALF)]
     remote(whole, whole, last_sems, other).wait_recv()
 
-    for copy in keep:
-        copy.wait()
     swap.wait_send()
     arrived.wait_send()
     remote(lines, lines, line_sems, other).wait_send()
@@ -162,19 +154,17 @@
     return pl.pallas_call(
         gram_kernel,
         out_shape=(
-            jax.ShapeDtypeStruct((2 * HALF, UNIT, 128), F32),
-            jax.ShapeDtypeStruct((ROWS, KEEP + NEW), BF16),
-            jax.ShapeDtypeStruct((ROWS, KEEP + NEW), BF16),
+            pltpu.VMEM((2 * HALF, UNIT, 128), F32),
+            pltpu.VMEM((ROWS, KEEP + NEW), BF16),
+            pltpu.VMEM((ROWS, KEEP + NEW), BF16),
         ),
         in_specs=[hbm] * 4,
-        out_specs=(vmem, hbm, hbm),
+        out_specs=(vmem, vmem, vmem),
         scratch_shapes=[
             pltpu.VMEM((ROWS, KEEP), F32),
             pltpu.VMEM((ROWS, NEW), F32),
             pltpu.VMEM((ROWS // 128, 128), F32),
             pltpu.VMEM((1, NEW), F32),
-            pltpu.VMEM((ROWS, KEEP + NEW), BF16),
-            pltpu.VMEM((ROWS, KEEP + NEW), BF16),
             pltpu.VMEM((2 * HALF, UNIT, 128), F32),
             pltpu.VMEM((HALF, UNIT, 128), F32),
             pltpu.VMEM(((PLANE - 1) * CHUNK, UNIT, 128), F32),
@@ -188,9 +178,10 @@
             pltpu.SemaphoreType.DMA((2,)),
             pltpu.SemaphoreType.DMA((PLANE,)),
             pltpu.SemaphoreType.DMA((2,)),
-            pltpu.SemaphoreType.DMA((2,)),
         ],
-        compiler_params=pltpu.CompilerParams(collective_id=0, has_side_effects=True),
+        compiler_params=pltpu.CompilerParams(
+            collective_id=0, has_side_effects=True, vmem_limit_bytes=VMEM_LIMIT
+        ),
         name="gram",
     )(trial, resid, energy.reshape(ROWS // 128, 128), shift.reshape(1, NEW))
 
@@ -198,10 +189,26 @@
 SIDE = 32
 
 
-def mul(left, right, dims):
-    return lax.dot_general(
-        left, right, ((dims[:1], dims[1:]), ((), ())), precision=lax.Precision.HIGHEST, preferred_element_type=F32
-    )
+def halves(value):
+    high = value.astype(BF16)
+    return high, (value - high.astype(F32)).astype(BF16)
+
+
+def dot(left, right):
+    return jnp.dot(left, right, preferred_element_type=F32)
+
+
+def mul(left, right):
+    wide = dot(left[0], jnp.concatenate(right, 1))
+    return wide[:, :NEW] + (wide[:, NEW:] + dot(left[1], right[0]))
+
+
+def square_of(v):
+    a, rest = v.astype(BF16), v
+    rest = rest - a.astype(F32)
+    b = rest.astype(BF16)
+    c = (rest - b.astype(F32)).astype(BF16)
+    return tdot(jnp.concatenate([a, a, a, b, b, c], 0), jnp.concatenate([a, b, c, a, b, a], 0))
 
 
 def inverse_factor(square, lane, row):
@@ -247,70 +254,76 @@
         if base + SIDE < NEW:
             left = rest.shape[0] - SIDE
             below = jnp.where(here[:left], 0.0, rest[SIDE:])
-            rest = below - mul(done, done, (0, 0))[base + SIDE:]
+            rest = below - square_of(done)[base + SIDE:]
     whole = jnp.concatenate(panels, 0)
     return jnp.where(lane <= row, whole, 0.0)
 
 
-def finish_kernel(count, total_ref, high_ref, low_ref, basis_ref, steady_ref, high, low, sems):
-    fetch = [
-        pltpu.make_async_copy(high_ref, high, sems.at[0]),
-        pltpu.make_async_copy(low_ref, low, sems.at[1]),
-    ]
-    for copy in fetch:
-        copy.start()
+def finish_kernel(count, total_ref, high, low, basis_ref, steady_ref, work, basis, sems):
     at = {
         pair: total_ref[n * 32:(n + 1) * 32].reshape(128, 128) * (1.0 / count) for n, pair in enumerate(PAIRS)
     }
-    metric = jnp.concatenate(
+    metric = halves(jnp.concatenate(
         [jnp.concatenate([at[i, j] if i <= j else at[j, i].T for j in range(3)], 1) for i in range(3)], 0
-    )
+    ))
     first = jnp.concatenate([at[i, 3] for i in range(3)], 0)
-    second = mul(metric, first, (1, 0))
-    third = mul(metric, second, (1, 0))
+    second = mul(metric, halves(first))
+    third = mul(metric, halves(second))
     coef = 2.0 * first - second
     image = 2.0 * second - third
-    square = at[3, 3] + mul(coef, image - 2.0 * first, (0, 0))
+    pair = halves(coef)
+    known = halves(image - 2.0 * first)
+    wide = tdot(pair[0], jnp.concatenate(known, 1))
+    square = at[3, 3] + (wide[:, :NEW] + (wide[:, NEW:] + tdot(pair[1], known[0])))
 
     lane = lax.broadcasted_iota(jnp.int32, (NEW, NEW), 1)
     row = lax.broadcasted_iota(jnp.int32, (NEW, NEW), 0)
+
     def on_diagonal(v):
         return jnp.sum(jnp.where(lane == row, v, 0.0), axis=0, keepdims=True)
-    terms = on_diagonal(at[3, 3]) + jnp.sum(jnp.abs(coef) * (2.0 * jnp.abs(first) + jnp.abs(image)), axis=0, keepdims=True)
-    steady = jnp.where(terms <= 16.0 * on_diagonal(square), 1.0, 0.0)
-    steady_ref[0, 0] = jnp.min(steady)
+
+    terms = on_diagonal(at[3, 3]) + jnp.sum(
+        jnp.abs(coef) * (2.0 * jnp.abs(first) + jnp.abs(image)), axis=0, keepdims=True
+    )
+    both = jnp.concatenate(pair, 1)
+    for r in range(0, ROWS, 256):
+        rows = slice(r, r + 256)
+        wide = dot(high[rows, :KEEP], both)
+        inside = wide[:, :NEW] + (wide[:, NEW:] + dot(low[rows, :KEEP], pair[0]))
+        block = (high[rows, KEEP:].astype(F32) - inside) + low[rows, KEEP:].astype(F32)
+        work[rows, :NEW], work[rows, NEW:] = halves(block)
 
     inverse = inverse_factor(square, lane, row)
-    tail = jnp.concatenate([-mul(coef, inverse, (1, 1)), inverse.T], 0)
-    tail_high = tail.astype(BF16)
-    tail_low = (tail - tail_high.astype(F32)).astype(BF16)
-    both = jnp.concatenate([tail_high, tail_low], 1)
-    for copy in fetch:
-        copy.wait()
-
-    def rows_of(b, _):
-        rows = pl.ds(pl.multiple_of(b * 256, 256), 256)
-        two = jnp.dot(high[rows, :], both, preferred_element_type=F32)
-        one = jnp.dot(low[rows, :], tail_high, preferred_element_type=F32)
-        basis_ref[rows, :] = two[:, :128] + (two[:, 128:] + one)
-        return _
-
-    lax.fori_loop(0, ROWS // 256, rows_of, 0)
+    steady = (terms <= 4.0 * on_diagonal(square)) & (on_diagonal(square) * on_diagonal(inverse) ** 2 <= 1000.0)
+    steady_ref[0, 0] = jnp.min(jnp.where(steady, 1.0, 0.0))
+    inverse = halves(inverse.T)
+    stack = jnp.concatenate(
+        [jnp.concatenate(inverse, 1), jnp.concatenate([inverse[0], jnp.zeros_like(inverse[0])], 1)], 0
+    )
+    stores = []
+    for n in range(4):
+        rows = pl.ds(n * (ROWS // 4), ROWS // 4)
+        wide = dot(work[rows, :], stack)
+        basis[rows, :] = wide[:, :NEW] + wide[:, NEW:]
+        stores.append(pltpu.make_async_copy(basis.at[rows], basis_ref.at[rows], sems.at[n]))
+        stores[-1].start()
+    for store in stores:
+        store.wait()
 
 
 def finish(total, high, low, count):
     vmem = pl.BlockSpec(memory_space=pltpu.VMEM)
-    hbm = pl.BlockSpec(memory_space=pl.ANY)
     return pl.pallas_call(
         lambda *refs: finish_kernel(count, *refs),
         out_shape=(jax.ShapeDtypeStruct((ROWS, NEW), F32), jax.ShapeDtypeStruct((1, 1), F32)),
-        in_specs=[vmem, hbm, hbm],
-        out_specs=(vmem, pl.BlockSpec(memory_space=pltpu.SMEM)),
+        in_specs=[vmem] * 3,
+        out_specs=(pl.BlockSpec(memory_space=pl.ANY), pl.BlockSpec(memory_space=pltpu.SMEM)),
         scratch_shapes=[
-            pltpu.VMEM((ROWS, KEEP + NEW), BF16),
-            pltpu.VMEM((ROWS, KEEP + NEW), BF16),
-            pltpu.SemaphoreType.DMA((2,)),
+            pltpu.VMEM((ROWS, 2 * NEW), BF16),
+            pltpu.VMEM((ROWS, NEW), F32),
+            pltpu.SemaphoreType.DMA((4,)),
         ],
+        compiler_params=pltpu.CompilerParams(vmem_limit_bytes=VMEM_LIMIT),
         name="finish",
     )(total, high, low)
 
@@ -372,8 +385,7 @@
         return nested_sum(v.reshape(-1), (("x", "core"), ("y", "z"))).reshape(v.shape)
 
     work = resid / (energy[:, None] - shift[None, :])
-    for sweep in range(2):
-        work = work - fdot(trial, total(fdot(trial.T, work)) / count)
+    work = lax.fori_loop(0, 2, lambda _, w: w - fdot(trial, total(fdot(trial.T, w)) / count), work)
     lower = jnp.linalg.cholesky(total(fdot(work.T, work)) / count)
     return jax.scipy.linalg.solve_triangular(lower, work.T, lower=True).T
 

time: 50.7 us -> 46.6 us (0.919)
  Pallas kernels: 49.4 us -> 45.3 us
    pallas_call x1, Pallas kernels: 9.75 us -> 6.23 us  [finish(): pl.pallas_call(lambda *refs: finish_kernel(count, *refs), out_shape=(jax....]
    pallas_call x1, Pallas kernels: 39.7 us -> 39.1 us  [gram(): pl.pallas_call(gram_kernel, out_shape=(pltpu.VMEM((2 * HALF, UNIT, 128),...]
where the time goes in v4:
time: 46.6 us; the launch traced here: 46.5 us
  Pallas kernels  45.3 us (97%)
  between operations  0.94 us (2%)
    pallas_call x1, Pallas kernels, gram(): pl.pallas_call(gram_kernel, out_shape=(pltpu.VMEM((2 * HALF, UNIT, 128),...  39.1 us
    pallas_call x1, Pallas kernels, finish(): pl.pallas_call(lambda *refs: finish_kernel(count, *refs), out_shape=(jax....  6.23 us

profile of v4, /device:TPU:1, one launch (start us, length us, event | category | flops | bytes accessed | tf_op | source)
XLA Modules:
  0.0 46.5 jit_solution(9072008919613622861)
XLA Ops:
  0.0 39.1 %gram.1 = (f32[320,4,128]{2,1,0:T(4,128)S(1)}, bf16[1536,512]{1,0:T(8,128)(2,1)S(1)}, bf16[1536,512]{1,0:T(8,128)(2,1)S(1)}) custom-call(f32[1536,384]{1,0:T(8,128)} %trial_ref.1, f32[1536,128]{1,0:T(8,128)} %resid_ref.1, f32[12,128]{1,0:T(8,128)} %bitcast.57, f32[1,128]{1,0:T(1,128)} %bitcast.60), custom_call_target="tpu_custom_call" | custom-call | tf_op jit(solution)/shard_map/gram/pallas_call | solution.py:154
  39.1 0.0 copy-start
  39.1 0.0 copy-start.1
  39.1 0.0 copy-start.2
  39.1 6.2 %finish.1 = (f32[1536,128]{1,0:T(8,128)}, f32[1,1]{1,0:T(1,128)}) custom-call(f32[320,4,128]{2,1,0:T(4,128)S(1)} %get-tuple-element.43.refs_0_, bf16[1536,512]{1,0:T(8,128)(2,1)S(1)} %get-tuple-element.44.refs_1_, bf16[1536,512]{1,0:T(8,128)(2,1)S(1)} %get-tuple-element.45.refs_2_), custom_call_target="tpu_custom_call" | custom-call | tf_op jit(solution)/shard_map/finish/pallas_call | solution.py:316
  46.1 0.0 copy-done
  46.1 0.0 copy-done.1
  46.1 0.0 copy-done.2
  46.1 0.2 conditional.1
Async XLA Ops:
  39.1 7.0 %copy-start = (f32[1536,384]{1,0:T(8,128)S(1)}, f32[1536,384]{1,0:T(8,128)}, u32[]{:S(2)}) copy-start(f32[1536,384]{1,0:T(8,128)} %trial_ref.1) | copy-start | bytes 7077892
  39.1 7.0 %copy-start.1 = (f32[1536]{0:T(1024)S(1)}, f32[1536]{0:T(1024)}, u32[]{:S(2)}) copy-start(f32[1536]{0:T(1024)} %param.10) | copy-start | bytes 18436
  39.1 7.0 %copy-start.2 = (f32[128]{0:T(128)S(1)}, f32[128]{0:T(128)}, u32[]{:S(2)}) copy-start(f32[128]{0:T(128)} %param.11) | copy-start | bytes 1540

commit v5 on v4

--- a/solution.py
+++ b/solution.py
@@ -15,9 +15,11 @@
 PAIRS = [(0, 0), (0, 1), (1, 1), (0, 2), (0, 3), (2, 2), (2, 3), (3, 3), (1, 2), (1, 3)]
 HALF = len(PAIRS) * 128 // UNIT // 2
 PLANE, LINE = 32, 8
-CHUNK = HALF // PLANE
+PIECES = ((0, 2), (2, 3))
+CHUNK = sum(size for _, size in PIECES)
 NEAR = [(i, j) for i in range(4) for j in range(8) if (i, j) != (0, 0)]
-FAR = sorted(NEAR, key=lambda o: -min(o[0], 4 - o[0]) - min(o[1], 8 - o[1]))
+ARRIVAL = sorted(NEAR, key=lambda o: min(o[0], 4 - o[0]) + min(o[1], 8 - o[1]))
+FAR = ARRIVAL[::-1]
 F32, BF16 = jnp.float32, jnp.bfloat16
 
 
@@ -30,6 +32,26 @@
     trial, resid, energy, shift, part, peer, held, own, line, done,
     load_sems, core_sems, plane_sems, line_sems, gather_sems, spread_sems, last_sems,
 ):
+    x, c = lax.axis_index("x"), lax.axis_index("core")
+    y, z = lax.axis_index("y"), lax.axis_index("z")
+    p = (1 - c) * y + c * z
+    q = (1 - c) * z + c * y
+    me = x * 8 + p
+    other = {"x": x, "core": 1 - c, "y": y, "z": z}
+    xs = [(x + i) % 4 for i in range(4)]
+    ps = [(p + j) % 8 for j in range(8)]
+    qs = [(q + j) % 8 for j in range(8)]
+
+    def in_plane(i, j):
+        return {"x": xs[i], "core": c, "y": (1 - c) * ps[j] + c * y, "z": (1 - c) * z + c * ps[j]}
+
+    def in_line(j):
+        return {"x": x, "core": c, "y": (1 - c) * y + c * qs[j], "z": (1 - c) * qs[j] + c * z}
+
+    barrier = pltpu.get_barrier_semaphore()
+    for device in [other] + [in_plane(i, j) for i, j in FAR] + [in_line(j) for j in range(1, 8)]:
+        pl.semaphore_signal(barrier, inc=1, device_id=device, device_id_type=MESH)
+
     loads = [
         pltpu.make_async_copy(energy_ref, energy, load_sems.at[0]),
         pltpu.make_async_copy(shift_ref, shift, load_sems.at[1]),
@@ -40,26 +62,6 @@
         loads.append(pltpu.make_async_copy(trial_ref.at[rows], trial.at[rows], load_sems.at[3 + 2 * b]))
     for load in loads:
         load.start()
-
-    x, c = lax.axis_index("x"), lax.axis_index("core")
-    y, z = lax.axis_index("y"), lax.axis_index("z")
-    p = (1 - c) * y + c * z
-    q = (1 - c) * z + c * y
-    me = x * 8 + p
-    other = {"x": x, "core": 1 - c, "y": y, "z": z}
-    xs = [(x + i) % 4 for i in range(4)]
-    ps = [(p + j) % 8 for j in range(8)]
-    qs = [(q + j) % 8 for j in range(8)]
-
-    def in_plane(i, j):
-        return {"x": xs[i], "core": c, "y": (1 - c) * ps[j] + c * y, "z": (1 - c) * z + c * ps[j]}
-
-    def in_line(j):
-        return {"x": x, "core": c, "y": (1 - c) * y + c * qs[j], "z": (1 - c) * qs[j] + c * z}
-
-    barrier = pltpu.get_barrier_semaphore()
-    for device in [other] + [in_plane(i, j) for i, j in FAR] + [in_line(j) for j in range(1, 8)]:
-        pl.semaphore_signal(barrier, inc=1, device_id=device, device_id_type=MESH)
 
     for b in range(ROWS // STEP):
         for load in loads[2 * b + 2:2 * b + 4] + (loads[:2] if b == 0 else []):
@@ -84,68 +86,91 @@
         for n, block in enumerate(blocks):
             part[pl.ds(h * HALF + n * 32, 32)] = block.reshape(32, UNIT, 128)
 
-    def remote(src, dst, sems, device):
+    def remote(src, dst, sems, n, device):
         return pltpu.make_async_remote_copy(
-            src_ref=src, dst_ref=dst, send_sem=sems.at[0], recv_sem=sems.at[1],
+            src_ref=src, dst_ref=dst, send_sem=sems.at[2 * n], recv_sem=sems.at[2 * n + 1],
             device_id=device, device_id_type=MESH,
         )
 
     mine, theirs = c * HALF, (1 - c) * HALF
+    started = []
     half(1 - c)
     pl.semaphore_wait(barrier, PLANE + LINE - 1)
-    swap = remote(part.at[pl.ds(theirs, HALF)], peer, core_sems, other)
-    swap.start()
+    swaps = [
+        remote(
+            part.at[pl.ds(theirs + at * PLANE, size * PLANE)], peer.at[pl.ds(at * PLANE, size * PLANE)],
+            core_sems, n, other,
+        )
+        for n, (at, size) in enumerate(PIECES)
+    ]
+    for swap in swaps:
+        swap.start()
     half(c)
-    swap.wait_recv()
-    peer[...] += part[pl.ds(mine, HALF)]
-
-    for n, (i, j) in enumerate(FAR):
-        k = xs[i] * 8 + ps[j]
-        remote(
-            peer.at[pl.ds(k * CHUNK, CHUNK)], held.at[pl.ds(n * CHUNK, CHUNK)], plane_sems, in_plane(i, j)
-        ).start()
-    arrived = remote(held, held, plane_sems, other)
-    arrived.wait_recv()
-    total = peer[pl.ds(me * CHUNK, CHUNK)]
-    for j in range(PLANE - 1):
-        total += held[j * CHUNK:(j + 1) * CHUNK]
-    own[...] = total
-    line[pl.ds(q * CHUNK, CHUNK)] = total
-
-    for j in (4, 3, 5, 2, 6, 1, 7):
-        remote(own, line.at[pl.ds(q * CHUNK, CHUNK)], line_sems, in_line(j)).start()
-    lines = line.at[pl.ds(0, (LINE - 1) * CHUNK)]
-    remote(lines, lines, line_sems, other).wait_recv()
-    total = line[0:CHUNK]
-    for j in range(1, LINE):
-        total += line[j * CHUNK:(j + 1) * CHUNK]
-    done[...] = total
-    total_ref[pl.ds(mine + me * CHUNK, CHUNK)] = total
-
-    def chunk_of(k):
-        return total_ref.at[pl.ds(mine + k * CHUNK, CHUNK)]
-
-    def spread(n, k, device):
+    for n, (at, size) in enumerate(PIECES):
+        swaps[n].wait_recv()
+        peer[at * PLANE:(at + size) * PLANE] += part[pl.ds(mine + at * PLANE, size * PLANE)]
+        for m, (i, j) in enumerate(FAR):
+            k = xs[i] * 8 + ps[j]
+            remote(
+                peer.at[pl.ds(at * PLANE + k * size, size)], held.at[pl.ds(at * (PLANE - 1) + m * size, size)],
+                plane_sems, n, in_plane(i, j),
+            ).start()
+
+    for n, (at, size) in enumerate(PIECES):
+        base = at * (PLANE - 1)
+        pieces = held.at[pl.ds(base, (PLANE - 1) * size)]
+        started.append(remote(pieces, pieces, plane_sems, n, other))
+        started[-1].wait_recv()
+        total = peer[pl.ds(at * PLANE + me * size, size)]
+        for m in range(PLANE - 1):
+            total += held[base + m * size:base + (m + 1) * size]
+        own[at:at + size] = total
+        spot = pl.ds(at * LINE + q * size, size)
+        line[spot] = total
+        for j in (4, 3, 5, 2, 6, 1, 7):
+            remote(own.at[pl.ds(at, size)], line.at[spot], line_sems, n, in_line(j)).start()
+
+    def chunk_of(n, k):
+        at, size = PIECES[n]
+        return total_ref.at[pl.ds(mine + at * PLANE + k * size, size)]
+
+    def spread(n, m, k, device):
         return pltpu.make_async_remote_copy(
-            src_ref=done, dst_ref=chunk_of(k), send_sem=gather_sems.at[0], recv_sem=spread_sems.at[n],
+            src_ref=done.at[pl.ds(*PIECES[n])], dst_ref=chunk_of(n, k),
+            send_sem=gather_sems.at[n], recv_sem=spread_sems.at[n * PLANE + m],
             device_id=device, device_id_type=MESH,
         )
 
-    for n, (i, j) in enumerate(NEAR):
-        spread(n, me, in_plane(i, j)).start()
-    remote(done, chunk_of(me), last_sems, other).start()
-    for n, (i, j) in enumerate(NEAR):
-        k = xs[-i % 4] * 8 + ps[-j % 8]
-        spread(n, k, other).wait_recv()
-        remote(chunk_of(k), chunk_of(k), last_sems, other).start()
+    for n, (at, size) in enumerate(PIECES):
+        lines = line.at[pl.ds(at * LINE, (LINE - 1) * size)]
+        started.append(remote(lines, lines, line_sems, n, other))
+        started[-1].wait_recv()
+        total = line[at * LINE:at * LINE + size]
+        for j in range(1, LINE):
+            total += line[at * LINE + j * size:at * LINE + (j + 1) * size]
+        done[at:at + size] = total
+        total_ref[pl.ds(mine + at * PLANE + me * size, size)] = total
+        for m, (i, j) in enumerate(NEAR):
+            spread(n, m, me, in_plane(i, j)).start()
+        remote(done.at[pl.ds(at, size)], chunk_of(n, me), last_sems, 0, other).start()
+
+    for n in range(len(PIECES)):
+        for i, j in ARRIVAL:
+            k = xs[-i % 4] * 8 + ps[-j % 8]
+            spread(n, NEAR.index((i, j)), k, other).wait_recv()
+            remote(chunk_of(n, k), chunk_of(n, k), last_sems, 0, other).start()
     whole = total_ref.at[pl.ds(theirs, HALF)]
-    remote(whole, whole, last_sems, other).wait_recv()
-
-    swap.wait_send()
-    arrived.wait_send()
-    remote(lines, lines, line_sems, other).wait_send()
-    remote(held, held, gather_sems, other).wait_send()
-    remote(whole, whole, last_sems, other).wait_send()
+    last = remote(whole, whole, last_sems, 0, other)
+    last.wait_recv()
+
+    for copy in (*swaps, *started, last):
+        copy.wait_send()
+    for n, (at, size) in enumerate(PIECES):
+        pieces = held.at[pl.ds(0, (PLANE - 1) * size)]
+        pltpu.make_async_remote_copy(
+            src_ref=pieces, dst_ref=pieces, send_sem=gather_sems.at[n], recv_sem=spread_sems.at[0],
+            device_id=other, device_id_type=MESH,
+        ).wait_send()
 
 
 def gram(trial, resid, energy, shift):
@@ -172,11 +197,11 @@
             pltpu.VMEM((LINE * CHUNK, UNIT, 128), F32),
             pltpu.VMEM((CHUNK, UNIT, 128), F32),
             pltpu.SemaphoreType.DMA((2 + 2 * ROWS // STEP,)),
-            pltpu.SemaphoreType.DMA((2,)),
-            pltpu.SemaphoreType.DMA((2,)),
-            pltpu.SemaphoreType.DMA((2,)),
-            pltpu.SemaphoreType.DMA((2,)),
-            pltpu.SemaphoreType.DMA((PLANE,)),
+            pltpu.SemaphoreType.DMA((2 * len(PIECES),)),
+            pltpu.SemaphoreType.DMA((2 * len(PIECES),)),
+            pltpu.SemaphoreType.DMA((2 * len(PIECES),)),
+            pltpu.SemaphoreType.DMA((len(PIECES),)),
+            pltpu.SemaphoreType.DMA((PLANE * len(PIECES),)),
             pltpu.SemaphoreType.DMA((2,)),
         ],
         compiler_params=pltpu.CompilerParams(
@@ -315,7 +340,7 @@
     vmem = pl.BlockSpec(memory_space=pltpu.VMEM)
     return pl.pallas_call(
         lambda *refs: finish_kernel(count, *refs),
-        out_shape=(jax.ShapeDtypeStruct((ROWS, NEW), F32), jax.ShapeDtypeStruct((1, 1), F32)),
+        out_shape=(jax.ShapeDtypeStruct((ROWS, NEW), F32), pltpu.SMEM((1, 1), F32)),
         in_specs=[vmem] * 3,
         out_specs=(pl.BlockSpec(memory_space=pl.ANY), pl.BlockSpec(memory_space=pltpu.SMEM)),
         scratch_shapes=[

time: 46.6 us -> 45.7 us (0.981)
  between operations: 0.94 us -> 0.25 us
    pallas_call x1, Pallas kernels: 6.23 us -> 5.71 us  [finish(): pl.pallas_call(lambda *refs: finish_kernel(count, *refs), out_shape=(jax....]
where the time goes in v5:
time: 45.7 us; the launch traced here: 45.5 us
  Pallas kernels  45 us (98%)
    pallas_call x1, Pallas kernels, gram(): pl.pallas_call(gram_kernel, out_shape=(pltpu.VMEM((2 * HALF, UNIT, 128),...  39.3 us
    pallas_call x1, Pallas kernels, finish(): pl.pallas_call(lambda *refs: finish_kernel(count, *refs), out_shape=(jax....  5.71 us

profile of v5, /device:TPU:1, one launch (start us, length us, event | category | flops | bytes accessed | tf_op | source)
XLA Modules:
  0.0 45.5 jit_solution(7046577038535802366)
XLA Ops:
  0.0 39.3 %gram.1 = (f32[320,4,128]{2,1,0:T(4,128)S(1)}, bf16[1536,512]{1,0:T(8,128)(2,1)S(1)}, bf16[1536,512]{1,0:T(8,128)(2,1)S(1)}) custom-call(f32[1536,384]{1,0:T(8,128)} %trial_ref.1, f32[1536,128]{1,0:T(8,128)} %resid_ref.1, f32[12,128]{1,0:T(8,128)} %bitcast.57, f32[1,128]{1,0:T(1,128)} %bitcast.60), custom_call_target="tpu_custom_call" | custom-call | tf_op jit(solution)/shard_map/gram/pallas_call | solution.py:179
  39.3 0.0 copy-start
  39.4 0.0 copy-start.1
  39.4 0.0 copy-start.2
  39.4 5.7 %finish.1 = (f32[1536,128]{1,0:T(8,128)}, f32[1,1]{1,0:T(1,128)S(4)}) custom-call(f32[320,4,128]{2,1,0:T(4,128)S(1)} %get-tuple-element.43.refs_0_, bf16[1536,512]{1,0:T(8,128)(2,1)S(1)} %get-tuple-element.44.refs_1_, bf16[1536,512]{1,0:T(8,128)(2,1)S(1)} %get-tuple-element.45.refs_2_), custom_call_target="tpu_custom_call" | custom-call | tf_op jit(solution)/shard_map/finish/pallas_call | solution.py:341
  45.1 0.0 copy-done
  45.1 0.0 copy-done.1
  45.1 0.0 copy-done.2
  45.1 0.2 conditional.1
Async XLA Ops:
  39.3 5.8 %copy-start = (f32[1536,384]{1,0:T(8,128)S(1)}, f32[1536,384]{1,0:T(8,128)}, u32[]{:S(2)}) copy-start(f32[1536,384]{1,0:T(8,128)} %trial_ref.1) | copy-start | bytes 7077892
  39.4 5.8 %copy-start.1 = (f32[1536]{0:T(1024)S(1)}, f32[1536]{0:T(1024)}, u32[]{:S(2)}) copy-start(f32[1536]{0:T(1024)} %param.10) | copy-start | bytes 18436
  39.4 5.8 %copy-start.2 = (f32[128]{0:T(128)S(1)}, f32[128]{0:T(128)}, u32[]{:S(2)}) copy-start(f32[128]{0:T(128)} %param.11) | copy-start | bytes 1540

commit v6 on v5

--- a/solution.py
+++ b/solution.py
@@ -211,7 +211,7 @@
     )(trial, resid, energy.reshape(ROWS // 128, 128), shift.reshape(1, NEW))
 
 
-SIDE = 32
+SIDE = 16
 
 
 def halves(value):
@@ -237,21 +237,21 @@
 
 
 def inverse_factor(square, lane, row):
-    tiles = SIDE // 8
-    sub = row[:8]
-    panels = []
-    rest = square
-    for base in range(0, NEW, SIDE):
+    lane, sub = lane[:8], row[:8]
+    count, own = NEW // 8, SIDE // 8
+    tiles = [square[t * 8:t * 8 + 8] for t in range(count)]
+    for first in range(0, count, own):
+        base, window = first * 8, range(min(2 * own, count - first))
         here = (lane >= base) & (lane < base + SIDE)
-        top = rest[:SIDE]
         cols = [
-            [jnp.broadcast_to(top[t * 8:t * 8 + 8, base + j:base + j + 1], (8, 128)) if t >= j // 8 else None
-             for t in range(tiles)]
+            [jnp.broadcast_to(tiles[first + t][:, base + j:base + j + 1], (8, 128)) if t >= j // 8 else None
+             for t in window]
             for j in range(SIDE)
         ]
-        unit = jnp.where(lane[:SIDE] == row[:SIDE] + base, 1.0, 0.0)
-        panel = jnp.where(here[:SIDE], unit, top)
-        panel = [panel[t * 8:t * 8 + 8] for t in range(tiles)]
+        panel = [
+            jnp.where(here, jnp.where(lane == sub + base + 8 * t, 1.0, 0.0) if t < own else 0.0, tiles[first + t])
+            for t in window
+        ]
         for k in range(SIDE):
             tk, sk = k // 8, k % 8
             pivot = jnp.broadcast_to(cols[k][tk][sk:sk + 1], (8, 128))
@@ -260,28 +260,26 @@
                 tn, sn = (k + 1) // 8, (k + 1) % 8
                 line = jnp.broadcast_to(cols[k][tn][sn:sn + 1], (8, 128))
                 ratio = scale * scale
-                for t in range(tn, tiles):
+                for t in window[tn:]:
                     cols[k + 1][t] = cols[k + 1][t] - (cols[k][t] * line) * ratio
-            for t in range(tk, tiles):
+            for t in window[tk:]:
                 cols[k][t] = cols[k][t] * scale
             line = jnp.broadcast_to(panel[tk][sk:sk + 1], (8, 128)) * scale
             panel[tk] = jnp.where(
                 sub == sk, line, panel[tk] - jnp.where(sub > sk, cols[k][tk], 0.0) * line
             )
-            for t in range(tk + 1, tiles):
+            for t in window[tk + 1:]:
                 panel[t] = panel[t] - cols[k][t] * line
             for j in range(k + 2, SIDE):
                 line = jnp.broadcast_to(cols[k][j // 8][j % 8:j % 8 + 1], (8, 128))
-                for t in range(j // 8, tiles):
+                for t in window[j // 8:]:
                     cols[j][t] = cols[j][t] - cols[k][t] * line
-        done = jnp.concatenate(panel, 0)
-        panels.append(done)
-        if base + SIDE < NEW:
-            left = rest.shape[0] - SIDE
-            below = jnp.where(here[:left], 0.0, rest[SIDE:])
-            rest = below - square_of(done)[base + SIDE:]
-    whole = jnp.concatenate(panels, 0)
-    return jnp.where(lane <= row, whole, 0.0)
+        tiles[first:first + len(window)] = panel
+        if first + 2 * own < count:
+            update = square_of(jnp.concatenate(panel[:own], 0))
+            for t in range(first + 2 * own, count):
+                tiles[t] = jnp.where(here, 0.0, tiles[t]) - update[t * 8:t * 8 + 8]
+    return jnp.where(lane[:1] <= row[:, :1], jnp.concatenate(tiles, 0), 0.0)
 
 
 def finish_kernel(count, total_ref, high, low, basis_ref, steady_ref, work, basis, sems):
@@ -310,6 +308,8 @@
     terms = on_diagonal(at[3, 3]) + jnp.sum(
         jnp.abs(coef) * (2.0 * jnp.abs(first) + jnp.abs(image)), axis=0, keepdims=True
     )
+    inverse = inverse_factor(square, lane, row)
+
     both = jnp.concatenate(pair, 1)
     for r in range(0, ROWS, 256):
         rows = slice(r, r + 256)
@@ -318,7 +318,6 @@
         block = (high[rows, KEEP:].astype(F32) - inside) + low[rows, KEEP:].astype(F32)
         work[rows, :NEW], work[rows, NEW:] = halves(block)
 
-    inverse = inverse_factor(square, lane, row)
     steady = (terms <= 4.0 * on_diagonal(square)) & (on_diagonal(square) * on_diagonal(inverse) ** 2 <= 1000.0)
     steady_ref[0, 0] = jnp.min(jnp.where(steady, 1.0, 0.0))
     inverse = halves(inverse.T)

time: 45.7 us -> 44.9 us (0.982)
  Pallas kernels: 45 us -> 44.3 us
    pallas_call x1, Pallas kernels: 5.71 us -> 4.98 us  [finish(): pl.pallas_call(lambda *refs: finish_kernel(count, *refs), out_shape=(jax....]
where the time goes in v6:
time: 44.9 us; the launch traced here: 44.8 us
  Pallas kernels  44.3 us (99%)
    pallas_call x1, Pallas kernels, gram(): pl.pallas_call(gram_kernel, out_shape=(pltpu.VMEM((2 * HALF, UNIT, 128),...  39.3 us
    pallas_call x1, Pallas kernels, finish(): pl.pallas_call(lambda *refs: finish_kernel(count, *refs), out_shape=(jax....  4.98 us

profile of v6, /device:TPU:1, one launch (start us, length us, event | category | flops | bytes accessed | tf_op | source)
XLA Modules:
  0.0 44.8 jit_solution(12531449380020995719)
XLA Ops:
  0.0 39.3 %gram.1 = (f32[320,4,128]{2,1,0:T(4,128)S(1)}, bf16[1536,512]{1,0:T(8,128)(2,1)S(1)}, bf16[1536,512]{1,0:T(8,128)(2,1)S(1)}) custom-call(f32[1536,384]{1,0:T(8,128)} %trial_ref.1, f32[1536,128]{1,0:T(8,128)} %resid_ref.1, f32[12,128]{1,0:T(8,128)} %bitcast.57, f32[1,128]{1,0:T(1,128)} %bitcast.60), custom_call_target="tpu_custom_call" | custom-call | tf_op jit(solution)/shard_map/gram/pallas_call | solution.py:179
  39.3 0.0 copy-start
  39.4 0.0 copy-start.1
  39.4 0.0 copy-start.2
  39.4 5.0 %finish.1 = (f32[1536,128]{1,0:T(8,128)}, f32[1,1]{1,0:T(1,128)S(4)}) custom-call(f32[320,4,128]{2,1,0:T(4,128)S(1)} %get-tuple-element.43.refs_0_, bf16[1536,512]{1,0:T(8,128)(2,1)S(1)} %get-tuple-element.44.refs_1_, bf16[1536,512]{1,0:T(8,128)(2,1)S(1)} %get-tuple-element.45.refs_2_), custom_call_target="tpu_custom_call" | custom-call | tf_op jit(solution)/shard_map/finish/pallas_call | solution.py:340
  44.4 0.0 copy-done
  44.4 0.0 copy-done.1
  44.4 0.0 copy-done.2
  44.4 0.2 conditional.1
Async XLA Ops:
  39.3 5.0 %copy-start = (f32[1536,384]{1,0:T(8,128)S(1)}, f32[1536,384]{1,0:T(8,128)}, u32[]{:S(2)}) copy-start(f32[1536,384]{1,0:T(8,128)} %trial_ref.1) | copy-start | bytes 7077892
  39.4 5.0 %copy-start.1 = (f32[1536]{0:T(1024)S(1)}, f32[1536]{0:T(1024)}, u32[]{:S(2)}) copy-start(f32[1536]{0:T(1024)} %param.10) | copy-start | bytes 18436
  39.4 5.0 %copy-start.2 = (f32[128]{0:T(128)S(1)}, f32[128]{0:T(128)}, u32[]{:S(2)}) copy-start(f32[128]{0:T(128)} %param.11) | copy-start | bytes 1540

commit v7 on v6

--- a/solution.py
+++ b/solution.py
@@ -12,11 +12,11 @@
 STEP = 384
 VMEM_LIMIT = 24 * 2**20
 UNIT = 4
-PAIRS = [(0, 0), (0, 1), (1, 1), (0, 2), (0, 3), (2, 2), (2, 3), (3, 3), (1, 2), (1, 3)]
-HALF = len(PAIRS) * 128 // UNIT // 2
+MAIN = 4 * 128 // UNIT
+HALF = MAIN + 1
 PLANE, LINE = 32, 8
-PIECES = ((0, 2), (2, 3))
-CHUNK = sum(size for _, size in PIECES)
+PIECES = ((0, 2), (2, 2))
+CHUNK = MAIN // PLANE
 NEAR = [(i, j) for i in range(4) for j in range(8) if (i, j) != (0, 0)]
 ARRIVAL = sorted(NEAR, key=lambda o: min(o[0], 4 - o[0]) + min(o[1], 8 - o[1]))
 FAR = ARRIVAL[::-1]
@@ -31,6 +31,7 @@
     trial_ref, resid_ref, energy_ref, shift_ref, total_ref, hi, lo,
     trial, resid, energy, shift, part, peer, held, own, line, done,
     load_sems, core_sems, plane_sems, line_sems, gather_sems, spread_sems, last_sems,
+    held_extra, own_extra, line_extra, done_extra, extra_sems,
 ):
     x, c = lax.axis_index("x"), lax.axis_index("core")
     y, z = lax.axis_index("y"), lax.axis_index("z")
@@ -82,7 +83,12 @@
         full = tdot(left, left) + (cross + cross.T)
         left = hi[:, thin]
         side = tdot(left, hi[:, 256:]) + (tdot(left, lo[:, 256:]) + tdot(lo[:, thin], hi[:, 256:]))
-        blocks = (full[:128, :128], full[:128, 128:], full[128:, 128:], side[:, :128], side[:, 128:])
+        lane = lax.broadcasted_iota(jnp.int32, (128, 128), 1)
+        row = lax.broadcasted_iota(jnp.int32, (128, 128), 0)
+        packed = jnp.where(lane >= row, full[:128, :128], full[128:, 128:])
+        diagonal = jnp.sum(jnp.where(lane == row, full[128:, 128:], 0.0), axis=0, keepdims=True)
+        part[pl.ds(h * HALF + MAIN, 1)] = jnp.broadcast_to(diagonal, (UNIT, 128)).reshape(1, UNIT, 128)
+        blocks = (packed, full[:128, 128:], side[:, :128], side[:, 128:])
         for n, block in enumerate(blocks):
             part[pl.ds(h * HALF + n * 32, 32)] = block.reshape(32, UNIT, 128)
 
@@ -98,7 +104,7 @@
     pl.semaphore_wait(barrier, PLANE + LINE - 1)
     swaps = [
         remote(
-            part.at[pl.ds(theirs + at * PLANE, size * PLANE)], peer.at[pl.ds(at * PLANE, size * PLANE)],
+            part.at[pl.ds(theirs + at * PLANE, size * PLANE + n)], peer.at[pl.ds(at * PLANE, size * PLANE + n)],
             core_sems, n, other,
         )
         for n, (at, size) in enumerate(PIECES)
@@ -108,13 +114,23 @@
     half(c)
     for n, (at, size) in enumerate(PIECES):
         swaps[n].wait_recv()
-        peer[at * PLANE:(at + size) * PLANE] += part[pl.ds(mine + at * PLANE, size * PLANE)]
+        peer[at * PLANE:(at + size) * PLANE + n] += part[pl.ds(mine + at * PLANE, size * PLANE + n)]
         for m, (i, j) in enumerate(FAR):
             k = xs[i] * 8 + ps[j]
             remote(
                 peer.at[pl.ds(at * PLANE + k * size, size)], held.at[pl.ds(at * (PLANE - 1) + m * size, size)],
                 plane_sems, n, in_plane(i, j),
             ).start()
+
+    spot_extra = total_ref.at[pl.ds(mine + MAIN, 1)]
+    to_first = remote(
+        peer.at[pl.ds(MAIN, 1)], held_extra.at[pl.ds((me + PLANE - 1) % PLANE, 1)], extra_sems, 0,
+        {"x": 0, "core": c, "y": c * y, "z": (1 - c) * z},
+    )
+
+    @pl.when(me != 0)
+    def _():
+        to_first.start()
 
     for n, (at, size) in enumerate(PIECES):
         base = at * (PLANE - 1)
@@ -130,6 +146,20 @@
         for j in (4, 3, 5, 2, 6, 1, 7):
             remote(own.at[pl.ds(at, size)], line.at[spot], line_sems, n, in_line(j)).start()
 
+    all_extra = held_extra.at[pl.ds(0, PLANE - 1)]
+    lines_extra = line_extra.at[pl.ds(0, LINE - 1)]
+
+    @pl.when(me == 0)
+    def _():
+        remote(all_extra, all_extra, extra_sems, 0, other).wait_recv()
+        total = peer[MAIN:MAIN + 1]
+        for m in range(PLANE - 1):
+            total += held_extra[m:m + 1]
+        own_extra[...] = total
+        line_extra[pl.ds(q, 1)] = total
+        for j in range(1, LINE):
+            remote(own_extra, line_extra.at[pl.ds(q, 1)], extra_sems, 1, in_line(j)).start()
+
     def chunk_of(n, k):
         at, size = PIECES[n]
         return total_ref.at[pl.ds(mine + at * PLANE + k * size, size)]
@@ -154,17 +184,44 @@
             spread(n, m, me, in_plane(i, j)).start()
         remote(done.at[pl.ds(at, size)], chunk_of(n, me), last_sems, 0, other).start()
 
+    @pl.when(me == 0)
+    def _():
+        remote(lines_extra, lines_extra, extra_sems, 1, other).wait_recv()
+        total = line_extra[0:1]
+        for j in range(1, LINE):
+            total += line_extra[j:j + 1]
+        done_extra[...] = total
+        total_ref[pl.ds(mine + MAIN, 1)] = total
+        for i, j in NEAR:
+            remote(done_extra, spot_extra, extra_sems, 2, in_plane(i, j)).start()
+        remote(done_extra, spot_extra, last_sems, 0, other).start()
+
     for n in range(len(PIECES)):
         for i, j in ARRIVAL:
             k = xs[-i % 4] * 8 + ps[-j % 8]
             spread(n, NEAR.index((i, j)), k, other).wait_recv()
             remote(chunk_of(n, k), chunk_of(n, k), last_sems, 0, other).start()
+
+    @pl.when(me != 0)
+    def _():
+        remote(done_extra, spot_extra, extra_sems, 2, other).wait_recv()
+        remote(spot_extra, spot_extra, last_sems, 0, other).start()
+
     whole = total_ref.at[pl.ds(theirs, HALF)]
     last = remote(whole, whole, last_sems, 0, other)
     last.wait_recv()
 
     for copy in (*swaps, *started, last):
         copy.wait_send()
+    @pl.when(me != 0)
+    def _():
+        to_first.wait_send()
+
+    @pl.when(me == 0)
+    def _():
+        remote(lines_extra, lines_extra, extra_sems, 1, other).wait_send()
+        remote(all_extra, all_extra, extra_sems, 2, other).wait_send()
+
     for n, (at, size) in enumerate(PIECES):
         pieces = held.at[pl.ds(0, (PLANE - 1) * size)]
         pltpu.make_async_remote_copy(
@@ -203,6 +260,11 @@
             pltpu.SemaphoreType.DMA((len(PIECES),)),
             pltpu.SemaphoreType.DMA((PLANE * len(PIECES),)),
             pltpu.SemaphoreType.DMA((2,)),
+            pltpu.VMEM((PLANE, UNIT, 128), F32),
+            pltpu.VMEM((1, UNIT, 128), F32),
+            pltpu.VMEM((LINE, UNIT, 128), F32),
+            pltpu.VMEM((1, UNIT, 128), F32),
+            pltpu.SemaphoreType.DMA((6,)),
         ],
         compiler_params=pltpu.CompilerParams(
             collective_id=0, has_side_effects=True, vmem_limit_bytes=VMEM_LIMIT
@@ -283,9 +345,18 @@
 
 
 def finish_kernel(count, total_ref, high, low, basis_ref, steady_ref, work, basis, sems):
-    at = {
-        pair: total_ref[n * 32:(n + 1) * 32].reshape(128, 128) * (1.0 / count) for n, pair in enumerate(PAIRS)
-    }
+    lane = lax.broadcasted_iota(jnp.int32, (NEW, NEW), 1)
+    row = lax.broadcasted_iota(jnp.int32, (NEW, NEW), 0)
+    at = {}
+    for h in range(2):
+        packed, *others = [
+            total_ref[h * HALF + n * 32:h * HALF + n * 32 + 32].reshape(128, 128) * (1.0 / count) for n in range(4)
+        ]
+        diagonal = total_ref[h * HALF + MAIN, 0:1, :] * (1.0 / count)
+        turned = packed.T
+        at[2 * h, 2 * h] = jnp.where(lane >= row, packed, turned)
+        at[2 * h + 1, 2 * h + 1] = jnp.where(lane < row, packed, jnp.where(lane > row, turned, diagonal))
+        at[2 * h, 2 * h + 1], at[h, 2], at[h, 3] = others
     metric = halves(jnp.concatenate(
         [jnp.concatenate([at[i, j] if i <= j else at[j, i].T for j in range(3)], 1) for i in range(3)], 0
     ))
@@ -298,9 +369,6 @@
     known = halves(image - 2.0 * first)
     wide = tdot(pair[0], jnp.concatenate(known, 1))
     square = at[3, 3] + (wide[:, :NEW] + (wide[:, NEW:] + tdot(pair[1], known[0])))
-
-    lane = lax.broadcasted_iota(jnp.int32, (NEW, NEW), 1)
-    row = lax.broadcasted_iota(jnp.int32, (NEW, NEW), 0)
 
     def on_diagonal(v):
         return jnp.sum(jnp.where(lane == row, v, 0.0), axis=0, keepdims=True)

time: 44.9 us -> 43.7 us (0.973)
  Pallas kernels: 44.3 us -> 43.1 us
    pallas_call x1, Pallas kernels: 39.3 us -> 38.2 us  [gram(): pl.pallas_call(gram_kernel, out_shape=(pltpu.VMEM((2 * HALF, UNIT, 128),...]
where the time goes in v7:
time: 43.7 us; the launch traced here: 43.6 us
  Pallas kernels  43.1 us (99%)
    pallas_call x1, Pallas kernels, gram(): pl.pallas_call(gram_kernel, out_shape=(pltpu.VMEM((2 * HALF, UNIT, 128),...  38.2 us
    pallas_call x1, Pallas kernels, finish(): pl.pallas_call(lambda *refs: finish_kernel(count, *refs), out_shape=(jax....  4.89 us

profile of v7, /device:TPU:1, one launch (start us, length us, event | category | flops | bytes accessed | tf_op | source)
XLA Modules:
  0.0 43.6 jit_solution(7169172591096992055)
XLA Ops:
  0.0 38.2 %gram.1 = (f32[258,4,128]{2,1,0:T(4,128)S(1)}, bf16[1536,512]{1,0:T(8,128)(2,1)S(1)}, bf16[1536,512]{1,0:T(8,128)(2,1)S(1)}) custom-call(f32[1536,384]{1,0:T(8,128)} %trial_ref.1, f32[1536,128]{1,0:T(8,128)} %resid_ref.1, f32[12,128]{1,0:T(8,128)} %bitcast.57, f32[1,128]{1,0:T(1,128)} %bitcast.60), custom_call_target="tpu_custom_call" | custom-call | tf_op jit(solution)/shard_map/gram/pallas_call | solution.py:236
  38.2 0.0 copy-start
  38.2 0.0 copy-start.1
  38.3 0.0 copy-start.2
  38.3 4.9 %finish.1 = (f32[1536,128]{1,0:T(8,128)}, f32[1,1]{1,0:T(1,128)S(4)}) custom-call(f32[258,4,128]{2,1,0:T(4,128)S(1)} %get-tuple-element.43.refs_0_, bf16[1536,512]{1,0:T(8,128)(2,1)S(1)} %get-tuple-element.44.refs_1_, bf16[1536,512]{1,0:T(8,128)(2,1)S(1)} %get-tuple-element.45.refs_2_), custom_call_target="tpu_custom_call" | custom-call | tf_op jit(solution)/shard_map/finish/pallas_call | solution.py:408
  43.2 0.0 copy-done
  43.2 0.0 copy-done.1
  43.2 0.0 copy-done.2
  43.2 0.2 conditional.1
Async XLA Ops:
  38.2 4.9 %copy-start = (f32[1536,384]{1,0:T(8,128)S(1)}, f32[1536,384]{1,0:T(8,128)}, u32[]{:S(2)}) copy-start(f32[1536,384]{1,0:T(8,128)} %trial_ref.1) | copy-start | bytes 7077892
  38.2 4.9 %copy-start.1 = (f32[1536]{0:T(1024)S(1)}, f32[1536]{0:T(1024)}, u32[]{:S(2)}) copy-start(f32[1536]{0:T(1024)} %param.10) | copy-start | bytes 18436
  38.3 4.9 %copy-start.2 = (f32[128]{0:T(128)S(1)}, f32[128]{0:T(128)}, u32[]{:S(2)}) copy-start(f32[128]{0:T(128)} %param.11) | copy-start | bytes 1540

commit v8 on v7

--- a/solution.py
+++ b/solution.py
@@ -11,11 +11,12 @@
 ROWS, KEEP, NEW = 1536, 384, 128
 STEP = 384
 VMEM_LIMIT = 24 * 2**20
-UNIT = 4
-MAIN = 4 * 128 // UNIT
+UNIT = 8
+BLOCK = 128 // UNIT
+MAIN = 4 * BLOCK
 HALF = MAIN + 1
 PLANE, LINE = 32, 8
-PIECES = ((0, 2), (2, 2))
+PIECES = ((0, 1), (1, 1))
 CHUNK = MAIN // PLANE
 NEAR = [(i, j) for i in range(4) for j in range(8) if (i, j) != (0, 0)]
 ARRIVAL = sorted(NEAR, key=lambda o: min(o[0], 4 - o[0]) + min(o[1], 8 - o[1]))
@@ -90,7 +91,7 @@
         part[pl.ds(h * HALF + MAIN, 1)] = jnp.broadcast_to(diagonal, (UNIT, 128)).reshape(1, UNIT, 128)
         blocks = (packed, full[:128, 128:], side[:, :128], side[:, 128:])
         for n, block in enumerate(blocks):
-            part[pl.ds(h * HALF + n * 32, 32)] = block.reshape(32, UNIT, 128)
+            part[pl.ds(h * HALF + n * BLOCK, BLOCK)] = block.reshape(BLOCK, UNIT, 128)
 
     def remote(src, dst, sems, n, device):
         return pltpu.make_async_remote_copy(
@@ -350,7 +351,8 @@
     at = {}
     for h in range(2):
         packed, *others = [
-            total_ref[h * HALF + n * 32:h * HALF + n * 32 + 32].reshape(128, 128) * (1.0 / count) for n in range(4)
+            total_ref[h * HALF + n * BLOCK:h * HALF + (n + 1) * BLOCK].reshape(128, 128) * (1.0 / count)
+            for n in range(4)
         ]
         diagonal = total_ref[h * HALF + MAIN, 0:1, :] * (1.0 / count)
         turned = packed.T

time: 43.7 us -> 43.7 us (level)
  no operation moved by 1% of the time
where the time goes in v8:
time: 43.7 us; the launch traced here: 43.6 us
  Pallas kernels  43.1 us (99%)
    pallas_call x1, Pallas kernels, gram(): pl.pallas_call(gram_kernel, out_shape=(pltpu.VMEM((2 * HALF, UNIT, 128),...  38.2 us
    pallas_call x1, Pallas kernels, finish(): pl.pallas_call(lambda *refs: finish_kernel(count, *refs), out_shape=(jax....  4.89 us

profile of v8, /device:TPU:1, one launch (start us, length us, event | category | flops | bytes accessed | tf_op | source)
XLA Modules:
  0.0 43.6 jit_solution(2967940080437316348)
XLA Ops:
  0.0 38.2 %gram.1 = (f32[130,8,128]{2,1,0:T(8,128)S(1)}, bf16[1536,512]{1,0:T(8,128)(2,1)S(1)}, bf16[1536,512]{1,0:T(8,128)(2,1)S(1)}) custom-call(f32[1536,384]{1,0:T(8,128)} %trial_ref.1, f32[1536,128]{1,0:T(8,128)} %resid_ref.1, f32[12,128]{1,0:T(8,128)} %bitcast.57, f32[1,128]{1,0:T(1,128)} %bitcast.60), custom_call_target="tpu_custom_call" | custom-call | tf_op jit(solution)/shard_map/gram/pallas_call | solution.py:237
  38.2 0.0 copy-start
  38.2 0.0 copy-start.1
  38.2 0.0 copy-start.2
  38.2 4.9 %finish.1 = (f32[1536,128]{1,0:T(8,128)}, f32[1,1]{1,0:T(1,128)S(4)}) custom-call(f32[130,8,128]{2,1,0:T(8,128)S(1)} %get-tuple-element.43.refs_0_, bf16[1536,512]{1,0:T(8,128)(2,1)S(1)} %get-tuple-element.44.refs_1_, bf16[1536,512]{1,0:T(8,128)(2,1)S(1)} %get-tuple-element.45.refs_2_), custom_call_target="tpu_custom_call" | custom-call | tf_op jit(solution)/shard_map/finish/pallas_call | solution.py:410
  43.1 0.0 copy-done
  43.2 0.0 copy-done.1
  43.2 0.0 copy-done.2
  43.2 0.2 conditional.1
Async XLA Ops:
  38.2 4.9 %copy-start = (f32[1536,384]{1,0:T(8,128)S(1)}, f32[1536,384]{1,0:T(8,128)}, u32[]{:S(2)}) copy-start(f32[1536,384]{1,0:T(8,128)} %trial_ref.1) | copy-start | bytes 7077892
  38.2 4.9 %copy-start.1 = (f32[1536]{0:T(1024)S(1)}, f32[1536]{0:T(1024)}, u32[]{:S(2)}) copy-start(f32[1536]{0:T(1024)} %param.10) | copy-start | bytes 18436
  38.2 4.9 %copy-start.2 = (f32[128]{0:T(128)S(1)}, f32[128]{0:T(128)}, u32[]{:S(2)}) copy-start(f32[128]{0:T(128)} %param.11) | copy-start | bytes 1540

commit v9 on v8

--- a/solution.py
+++ b/solution.py
@@ -102,6 +102,7 @@
     mine, theirs = c * HALF, (1 - c) * HALF
     started = []
     half(1 - c)
+    half(c)
     pl.semaphore_wait(barrier, PLANE + LINE - 1)
     swaps = [
         remote(
@@ -112,7 +113,6 @@
     ]
     for swap in swaps:
         swap.start()
-    half(c)
     for n, (at, size) in enumerate(PIECES):
         swaps[n].wait_recv()
         peer[at * PLANE:(at + size) * PLANE + n] += part[pl.ds(mine + at * PLANE, size * PLANE + n)]

time: 43.7 us -> 42.8 us (0.979)
  Pallas kernels: 43.1 us -> 42.2 us
    pallas_call x1, Pallas kernels: 38.2 us -> 37.3 us  [gram(): pl.pallas_call(gram_kernel, out_shape=(pltpu.VMEM((2 * HALF, UNIT, 128),...]
where the time goes in v9:
time: 42.8 us; the launch traced here: 42.7 us
  Pallas kernels  42.2 us (99%)
    pallas_call x1, Pallas kernels, gram(): pl.pallas_call(gram_kernel, out_shape=(pltpu.VMEM((2 * HALF, UNIT, 128),...  37.3 us
    pallas_call x1, Pallas kernels, finish(): pl.pallas_call(lambda *refs: finish_kernel(count, *refs), out_shape=(jax....  4.88 us

profile of v9, /device:TPU:1, one launch (start us, length us, event | category | flops | bytes accessed | tf_op | source)
XLA Modules:
  0.0 42.7 jit_solution(12490778334231062621)
XLA Ops:
  0.0 37.3 %gram.1 = (f32[130,8,128]{2,1,0:T(8,128)S(1)}, bf16[1536,512]{1,0:T(8,128)(2,1)S(1)}, bf16[1536,512]{1,0:T(8,128)(2,1)S(1)}) custom-call(f32[1536,384]{1,0:T(8,128)} %trial_ref.1, f32[1536,128]{1,0:T(8,128)} %resid_ref.1, f32[12,128]{1,0:T(8,128)} %bitcast.57, f32[1,128]{1,0:T(1,128)} %bitcast.60), custom_call_target="tpu_custom_call" | custom-call | tf_op jit(solution)/shard_map/gram/pallas_call | solution.py:237
  37.3 0.0 copy-start
  37.3 0.0 copy-start.1
  37.3 0.0 copy-start.2
  37.3 4.9 %finish.1 = (f32[1536,128]{1,0:T(8,128)}, f32[1,1]{1,0:T(1,128)S(4)}) custom-call(f32[130,8,128]{2,1,0:T(8,128)S(1)} %get-tuple-element.43.refs_0_, bf16[1536,512]{1,0:T(8,128)(2,1)S(1)} %get-tuple-element.44.refs_1_, bf16[1536,512]{1,0:T(8,128)(2,1)S(1)} %get-tuple-element.45.refs_2_), custom_call_target="tpu_custom_call" | custom-call | tf_op jit(solution)/shard_map/finish/pallas_call | solution.py:410
  42.2 0.0 copy-done
  42.2 0.0 copy-done.1
  42.2 0.0 copy-done.2
  42.2 0.2 conditional.1
Async XLA Ops:
  37.3 4.9 %copy-start = (f32[1536,384]{1,0:T(8,128)S(1)}, f32[1536,384]{1,0:T(8,128)}, u32[]{:S(2)}) copy-start(f32[1536,384]{1,0:T(8,128)} %trial_ref.1) | copy-start | bytes 7077892
  37.3 4.9 %copy-start.1 = (f32[1536]{0:T(1024)S(1)}, f32[1536]{0:T(1024)}, u32[]{:S(2)}) copy-start(f32[1536]{0:T(1024)} %param.10) | copy-start | bytes 18436
  37.3 4.9 %copy-start.2 = (f32[128]{0:T(128)S(1)}, f32[128]{0:T(128)}, u32[]{:S(2)}) copy-start(f32[128]{0:T(128)} %param.11) | copy-start | bytes 1540

commit v10 on v9

--- a/solution.py
+++ b/solution.py
@@ -16,7 +16,7 @@
 MAIN = 4 * BLOCK
 HALF = MAIN + 1
 PLANE, LINE = 32, 8
-PIECES = ((0, 1), (1, 1))
+PIECES = ((0, 2),)
 CHUNK = MAIN // PLANE
 NEAR = [(i, j) for i in range(4) for j in range(8) if (i, j) != (0, 0)]
 ARRIVAL = sorted(NEAR, key=lambda o: min(o[0], 4 - o[0]) + min(o[1], 8 - o[1]))
@@ -106,7 +106,7 @@
     pl.semaphore_wait(barrier, PLANE + LINE - 1)
     swaps = [
         remote(
-            part.at[pl.ds(theirs + at * PLANE, size * PLANE + n)], peer.at[pl.ds(at * PLANE, size * PLANE + n)],
+            part.at[pl.ds(theirs + at * PLANE, size * PLANE + (n == len(PIECES) - 1))], peer.at[pl.ds(at * PLANE, size * PLANE + (n == len(PIECES) - 1))],
             core_sems, n, other,
         )
         for n, (at, size) in enumerate(PIECES)
@@ -115,7 +115,7 @@
         swap.start()
     for n, (at, size) in enumerate(PIECES):
         swaps[n].wait_recv()
-        peer[at * PLANE:(at + size) * PLANE + n] += part[pl.ds(mine + at * PLANE, size * PLANE + n)]
+        peer[at * PLANE:(at + size) * PLANE + (n == len(PIECES) - 1)] += part[pl.ds(mine + at * PLANE, size * PLANE + (n == len(PIECES) - 1))]
         for m, (i, j) in enumerate(FAR):
             k = xs[i] * 8 + ps[j]
             remote(

time: 42.8 us -> 42.2 us (0.986)
  Pallas kernels: 42.2 us -> 41.6 us
    pallas_call x1, Pallas kernels: 37.3 us -> 36.7 us  [gram(): pl.pallas_call(gram_kernel, out_shape=(pltpu.VMEM((2 * HALF, UNIT, 128),...]
where the time goes in v10:
time: 42.2 us; the launch traced here: 42.1 us
  Pallas kernels  41.6 us (99%)
    pallas_call x1, Pallas kernels, gram(): pl.pallas_call(gram_kernel, out_shape=(pltpu.VMEM((2 * HALF, UNIT, 128),...  36.7 us
    pallas_call x1, Pallas kernels, finish(): pl.pallas_call(lambda *refs: finish_kernel(count, *refs), out_shape=(jax....  4.88 us

profile of v10, /device:TPU:1, one launch (start us, length us, event | category | flops | bytes accessed | tf_op | source)
XLA Modules:
  0.0 42.1 jit_solution(8746339455532972183)
XLA Ops:
  0.0 36.7 %gram.1 = (f32[130,8,128]{2,1,0:T(8,128)S(1)}, bf16[1536,512]{1,0:T(8,128)(2,1)S(1)}, bf16[1536,512]{1,0:T(8,128)(2,1)S(1)}) custom-call(f32[1536,384]{1,0:T(8,128)} %trial_ref.1, f32[1536,128]{1,0:T(8,128)} %resid_ref.1, f32[12,128]{1,0:T(8,128)} %bitcast.57, f32[1,128]{1,0:T(1,128)} %bitcast.60), custom_call_target="tpu_custom_call" | custom-call | tf_op jit(solution)/shard_map/gram/pallas_call | solution.py:237
  36.7 0.0 copy-start
  36.7 0.0 copy-start.1
  36.7 0.0 copy-start.2
  36.7 4.9 %finish.1 = (f32[1536,128]{1,0:T(8,128)}, f32[1,1]{1,0:T(1,128)S(4)}) custom-call(f32[130,8,128]{2,1,0:T(8,128)S(1)} %get-tuple-element.43.refs_0_, bf16[1536,512]{1,0:T(8,128)(2,1)S(1)} %get-tuple-element.44.refs_1_, bf16[1536,512]{1,0:T(8,128)(2,1)S(1)} %get-tuple-element.45.refs_2_), custom_call_target="tpu_custom_call" | custom-call | tf_op jit(solution)/shard_map/finish/pallas_call | solution.py:410
  41.6 0.0 copy-done
  41.6 0.0 copy-done.1
  41.6 0.0 copy-done.2
  41.7 0.2 conditional.1
Async XLA Ops:
  36.7 4.9 %copy-start = (f32[1536,384]{1,0:T(8,128)S(1)}, f32[1536,384]{1,0:T(8,128)}, u32[]{:S(2)}) copy-start(f32[1536,384]{1,0:T(8,128)} %trial_ref.1) | copy-start | bytes 7077892
  36.7 4.9 %copy-start.1 = (f32[1536]{0:T(1024)S(1)}, f32[1536]{0:T(1024)}, u32[]{:S(2)}) copy-start(f32[1536]{0:T(1024)} %param.10) | copy-start | bytes 18436
  36.7 4.9 %copy-start.2 = (f32[128]{0:T(128)S(1)}, f32[128]{0:T(128)}, u32[]{:S(2)}) copy-start(f32[128]{0:T(128)} %param.11) | copy-start | bytes 1540
